TPU v7x, 256 devices: a whole 4x4x8 slice. The times are simulated.
256 devices in a mesh: blk: 256 (over z, y, x, core).
Axes of the slice: x: 4, y: 4, z: 8, core: 2. Of those that a mesh axis runs over, the one named last changes fastest.
Arguments:
- populations: float32 [1024, 27, 4096], P('blk'), may hold values from 0.6 to 1.4
- scalars: float32 [1024, 9, 4096], P('blk'), may hold values from 0 to 1
- coarse_old: float32 [1024, 27, 512], P('blk'), may hold values from 0.6 to 1.4
- coarse_new: float32 [1024, 27, 512], P('blk'), may hold values from 0.6 to 1.4
- levels: int32 [1024], replicated, may hold values 0 or 1
- neighbours: int32 [1024, 6], P('blk'), may hold values from 0 to 1023, as said below
- relax_rates: float32 [27], replicated, may hold values from 0.5 to 1.9
- diffusivity: float32 [9], replicated, may hold values from 0.02 to 0.15
- stoichiometry: float32 [9], replicated, may hold values from -1 to 1
Outputs:
- new_populations: float32 [1024, 27, 4096], P('blk')
- new_scalars: float32 [1024, 9, 4096], P('blk')
- coarse_return: float32 [1024, 3456], P('blk')
Inputs may be any that keep to these rules, and one draw needn't show every extreme that they name: `neighbours`: block k lies in slot k % 4 of device k // 4. The blocks 4 * 2 * L up to 4 * 2 * (L + 1) - 1 form layer L (0 <= L < 128), held by devices 2 L and 2 L + 1; the blocks beside a block of layer L on sides 0 to 3 lie in layer L, the one on side 4 in layer L - 1 and the one on side 5 in layer L + 1, taken modulo 128. The relation is symmetric: if m is beside k on side q, k is beside m on side q xor 1. Hence the device of every listed block is at most 3 devices from the device of block k, counting cyclically over all devices.
All inputs are finite; a program needn't handle non-finite values.
Results may differ from a plain program's by a relative error of at most 0.0001.
Values sent between devices are 32-bit elements; how exact they have to be, the bound alone decides.
No kernel may reach another device: no remote copies, remote signals or barrier semaphores. Data moves between devices by JAX's collectives and lax.ppermute only.
A program may use at most 128 MiB of HBM per device.

v0:
```python
import jax
import jax.numpy as jnp
import numpy as np
from jax import lax
from jax.sharding import PartitionSpec as P

BLOCK_EDGE = 16
HALF_EDGE = 8


PREFACTOR = 1.0
ZELDOVICH = 4.0


def shifted_2(shard, axis, by):
    devices = lax.axis_size(axis)
    return lax.ppermute(shard, axis, [(i, (i + by) % devices) for i in range(devices)])


def lattice_tables():
    steps_one = (-1.0, 0.0, 1.0)
    velocities = np.array([[a, b, c] for a in steps_one for b in steps_one for c in steps_one])
    weights = np.prod(np.where(velocities == 0, 2.0 / 3.0, 1.0 / 6.0), axis=1)
    vander = np.array([[1.0, 1.0, 1.0], [-1.0, 0.0, 1.0], [1.0, 0.0, 1.0]])
    moments = np.kron(np.kron(vander, vander), vander)
    inverse = np.array([[0.0, -0.5, 0.5], [1.0, 0.0, -1.0], [0.0, 0.5, 0.5]])
    inverse_moments = np.kron(np.kron(inverse, inverse), inverse)
    return (velocities, weights, moments, inverse_moments)


def relaxation(relax_rates):
    velocities, weights, moments, inverse_moments = lattice_tables()
    left_part = jnp.asarray(inverse_moments / weights[:, None], jnp.float32)
    right_part = jnp.asarray(moments * weights[None, :], jnp.float32)
    return jnp.dot(
        left_part * relax_rates[None, :],
        right_part,
        precision=lax.Precision.HIGHEST,
        preferred_element_type=jnp.float32,
    )


def moment_rows():
    velocities, weights, moments, inverse_moments = lattice_tables()
    return np.concatenate([weights[None, :], (velocities * weights[:, None]).T], axis=0)


def cell_stride(direction, extent):
    return extent ** (2 - direction)


def coordinate_of(direction, extent):
    return jnp.asarray(np.arange(extent**3) // cell_stride(direction, extent) % extent, jnp.int32)


def layer_of(flat, direction, upward, extent):
    index = (extent - 1) * upward
    last_axis = flat.ndim - 1
    lead = flat.shape[:-1]
    if direction == 0:
        return lax.slice_in_dim(
            flat, index * extent * extent, (index + 1) * extent * extent, axis=last_axis
        )
    if direction == 1:
        shaped = flat.reshape(lead + (extent, extent * extent))
        picked = lax.slice_in_dim(shaped, index * extent, (index + 1) * extent, axis=last_axis + 1)
        return picked.reshape(lead + (extent * extent,))
    return lax.slice_in_dim(flat, index, flat.shape[-1], stride=extent, axis=last_axis)


def spread_face(face, direction, extent):
    lead = face.shape[:-1]
    if direction == 0:
        return jnp.tile(face, (1,) * len(lead) + (extent,))
    if direction == 1:
        square_face = face.reshape(lead + (extent, extent))
        tiled = jnp.tile(square_face, (1,) * (len(lead) + 1) + (extent,))
        return tiled.reshape(lead + (extent**3,))
    return jnp.repeat(face, extent, axis=len(lead))


def move_up(flat, face, direction, extent):
    stride = cell_stride(direction, extent)
    lead = flat.shape[:-1]
    shifted = jnp.concatenate(
        [jnp.zeros(lead + (stride,), flat.dtype), flat[..., :-stride]], axis=len(lead)
    )
    return jnp.where(
        coordinate_of(direction, extent) == 0, spread_face(face, direction, extent), shifted
    )


def move_down(flat, face, direction, extent):
    stride = cell_stride(direction, extent)
    lead = flat.shape[:-1]
    shifted = jnp.concatenate(
        [flat[..., stride:], jnp.zeros(lead + (stride,), flat.dtype)], axis=len(lead)
    )
    return jnp.where(
        coordinate_of(direction, extent) == extent - 1,
        spread_face(face, direction, extent),
        shifted,
    )


def collide(lattice_state, operator_matrix):
    blocks = lattice_state.shape[0]
    velocities, weights, moments, inverse_moments = lattice_tables()
    flattened = lattice_state.reshape(blocks, 27, -1)
    moment_sums = jnp.einsum(
        "pi,bic->bpc",
        jnp.asarray(moment_rows(), jnp.float32),
        flattened,
        precision=lax.Precision.HIGHEST,
    )
    density = moment_sums[:, 0:1]
    current = moment_sums[:, 1:4]
    projected = jnp.einsum(
        "id,bdc->bic",
        jnp.asarray(velocities, jnp.float32),
        current,
        precision=lax.Precision.HIGHEST,
    )
    square = jnp.sum(current * current, axis=1, keepdims=True)
    balance = density + 3.0 * projected + 4.5 * projected * projected - 1.5 * square
    relaxed = flattened - jnp.einsum(
        "ik,bkc->bic", operator_matrix, flattened - balance, precision=lax.Precision.HIGHEST
    )
    return relaxed.reshape(lattice_state.shape)


def outgoing(relaxed, extent):
    blocks = relaxed.shape[0]
    halved = extent // 2
    face_list = []
    for facing in range(6):
        direction = facing // 2
        upward = facing % 2
        moving = lax.index_in_dim(relaxed, 2 * upward, 1 + direction, keepdims=False).reshape(
            blocks, 9, -1
        )
        layer_face = layer_of(moving, direction, upward, extent)
        grouped = layer_face.reshape(blocks, 9, halved, 2, halved, 2)
        merged = jnp.sum(grouped, axis=(3, 5)) * 0.25
        face_list.append(merged.reshape(blocks, 9, halved * halved))
    return jnp.stack(face_list, axis=1)


def enlarge(face_values, halved):
    blocks = face_values.shape[0]
    square_face = face_values.reshape(blocks, 9, halved, halved)
    grown = jnp.repeat(jnp.repeat(square_face, 2, axis=2), 2, axis=3)
    return grown.reshape(blocks, 9, 4 * halved * halved)


def crossing_faces(read, coarse_now, fine_mask, direction, extent, halved):
    blocks = read.shape[0]
    high_face = layer_of(
        lax.index_in_dim(read, 2, 1 + direction, False).reshape(blocks, 9, -1), direction, 1, extent
    )
    low_face = layer_of(
        lax.index_in_dim(read, 0, 1 + direction, False).reshape(blocks, 9, -1), direction, 0, extent
    )
    coarse_high = enlarge(
        layer_of(
            lax.index_in_dim(coarse_now, 2, 1 + direction, False).reshape(blocks, 9, -1),
            direction,
            1,
            halved,
        ),
        halved,
    )
    coarse_low = enlarge(
        layer_of(
            lax.index_in_dim(coarse_now, 0, 1 + direction, False).reshape(blocks, 9, -1),
            direction,
            0,
            halved,
        ),
        halved,
    )
    keep_fine = fine_mask[:, None, None]
    high_face = jnp.where(keep_fine, high_face, coarse_high)
    low_face = jnp.where(keep_fine, low_face, coarse_low)
    return jnp.stack([high_face, low_face], axis=1)


def apply_section(read, from_low, from_high, direction, extent):
    forward = lax.index_in_dim(read, 2, 1 + direction, False)
    backward = lax.index_in_dim(read, 0, 1 + direction, False)
    middle = lax.index_in_dim(read, 1, 1 + direction, False)
    forward = move_up(forward, from_low, direction, extent)
    backward = move_down(backward, from_high, direction, extent)
    return jnp.stack([backward, middle, forward], axis=1 + direction)


def species_rims(species, extent):
    rim_list = []
    for facing in range(6):
        rim_list.append(layer_of(species, facing // 2, facing % 2, extent))
    return jnp.stack(rim_list, axis=1)


def advance_species(species, read, halo_faces, diffusivity, stoichiometry, extent):
    blocks = species.shape[0]
    flattened = read.reshape(blocks, 27, -1)
    current = jnp.einsum(
        "pi,bic->bpc",
        jnp.asarray(moment_rows()[1:4], jnp.float32),
        flattened,
        precision=lax.Precision.HIGHEST,
    )
    drift_term = jnp.zeros_like(species)
    spread = jnp.zeros_like(species)
    for direction in range(3):
        upper_cells = move_down(species, halo_faces[:, 2 * direction + 1], direction, extent)
        lower_cells = move_up(species, halo_faces[:, 2 * direction], direction, extent)
        drift_term = drift_term + current[:, direction][:, None] * (upper_cells - lower_cells) * 0.5
        spread = spread + (upper_cells + lower_cells - 2.0 * species)
    burning = PREFACTOR * species[:, 0] * species[:, 1] * jnp.exp(ZELDOVICH * (species[:, 8] - 1.0))
    return (
        species
        - drift_term
        + diffusivity[None, :, None] * spread
        + stoichiometry[None, :, None] * burning[:, None]
    )


def send_section(payload, offset):
    return shifted_2(payload, "blk", offset)


def send_scalars(payload, offset):
    return shifted_2(payload, "blk", offset)


def send_returned(payload, offset):
    return shifted_2(payload, "blk", offset)


def collect(payload, sender, offsets_list):
    pieces = []
    for offset in offsets_list:
        pieces.append(payload if offset == 0 else sender(payload, offset))
    return jnp.stack(pieces, axis=0)


def side_values(table, sender, distance, positions, near_offsets):
    base = -near_offsets[0]
    nearby = collect(table[:, 0:4], sender, near_offsets)
    below = collect(table[:, 5], sender, (1, 2, 3))
    above = collect(table[:, 4], sender, (-1, -2, -3))
    values = [
        nearby[distance[:, facing] + base, positions[:, facing], facing ^ 1] for facing in range(4)
    ]
    values.append(below[distance[:, 4] - 1, positions[:, 4]])
    values.append(above[-distance[:, 5] - 1, positions[:, 5]])
    return values


def local(
    populations,
    scalars,
    coarse_old,
    coarse_new,
    levels,
    neighbours,
    relax_rates,
    diffusivity,
    stoichiometry,
):
    slot_count = populations.shape[0]
    extent = BLOCK_EDGE
    halved = HALF_EDGE
    devices = lax.axis_size("blk")
    device_index = lax.axis_index("blk")
    near_offsets = (-1, 0, 1)
    base = -near_offsets[0]
    own_levels = lax.dynamic_slice_in_dim(levels, device_index * slot_count, slot_count)
    fine_mask = own_levels == 1
    neighbour_fine = levels[neighbours] == 1
    owners = neighbours // slot_count
    positions = neighbours % slot_count
    distance = (device_index - owners) % devices
    distance = jnp.where(distance > devices // 2, distance - devices, distance)
    operator_matrix = relaxation(relax_rates)
    lattice_state = populations.reshape(slot_count, 3, 3, 3, -1)
    species = scalars
    old_coarse = coarse_old.reshape(slot_count, 3, 3, 3, -1)
    new_coarse = coarse_new.reshape(slot_count, 3, 3, 3, -1)
    returned = jnp.zeros((slot_count, 6, 9, halved * halved), jnp.float32)
    for substep in range(2):
        coarse_now = old_coarse if substep == 0 else 0.5 * (old_coarse + new_coarse)
        relaxed = collide(lattice_state, operator_matrix)
        returned = returned + 0.5 * jnp.where(
            fine_mask[:, None, None, None], outgoing(relaxed, extent), 0.0
        )
        read = relaxed
        for direction in range(3):
            low_column = 2 * direction
            high_column = low_column + 1
            table = crossing_faces(read, coarse_now, fine_mask, direction, extent, halved)
            if direction == 2:
                low_stack = collect(table[:, 0], send_section, (1, 2, 3))
                high_stack = collect(table[:, 1], send_section, (-1, -2, -3))
                from_low = low_stack[distance[:, low_column] - 1, positions[:, low_column]]
                from_high = high_stack[-distance[:, high_column] - 1, positions[:, high_column]]
            else:
                stacked = collect(table, send_section, near_offsets)
                from_low = stacked[distance[:, low_column] + base, positions[:, low_column], 0]
                from_high = stacked[distance[:, high_column] + base, positions[:, high_column], 1]
            from_low = from_low.reshape(slot_count, 3, 3, extent * extent)
            from_high = from_high.reshape(slot_count, 3, 3, extent * extent)
            read = apply_section(read, from_low, from_high, direction, extent)
        rim_faces = species_rims(species, extent)
        received_list = side_values(rim_faces, send_scalars, distance, positions, near_offsets)
        halo_list = []
        for facing in range(6):
            halo_list.append(
                jnp.where(
                    neighbour_fine[:, facing][:, None, None],
                    received_list[facing],
                    rim_faces[:, facing],
                )
            )
        species = advance_species(
            species, read, jnp.stack(halo_list, axis=1), diffusivity, stoichiometry, extent
        )
        lattice_state = read
    coarse_list = side_values(returned, send_returned, distance, positions, near_offsets)
    coarse_return = jnp.where(
        fine_mask[:, None, None, None], 0.0, jnp.stack(coarse_list, axis=1)
    ).reshape(slot_count, -1)
    new_populations = jnp.where(
        fine_mask[:, None, None], lattice_state.reshape(populations.shape), populations
    )
    new_scalars = jnp.where(fine_mask[:, None, None], species, scalars)
    return (new_populations, new_scalars, coarse_return)


def solution(mesh):
    in_specs = (
        P("blk", None, None),
        P("blk", None, None),
        P("blk", None, None),
        P("blk", None, None),
        P(),
        P("blk", None),
        P(),
        P(),
        P(),
    )
    out_specs = (P("blk", None, None), P("blk", None, None), P("blk", None))
    return jax.shard_map(local, mesh=mesh, in_specs=in_specs, out_specs=out_specs, check_vma=False)
```

profile of v0, /device:TPU:1, one launch (start us, length us, event | category | flops | bytes accessed | tf_op | source)
XLA Modules:
  0.0 583.7 jit_solution(5746134281485587863)
XLA Ops:
  3.8 11.6 %collective-permute-start.24 = (f32[4,9,256]{2,0,1:T(4,128)}, f32[4,9,256]{2,0,1:T(4,128)}, u32[]{:S(2)}, u32[]{:S(2)}) collective-permute-start(f32[4,9,256]{2,0,1:T(4,128)} %slice.601), channel_id=1, source_target_pairs={{0,253},{1,254},{2,255},{3,0},{4,1},{5,2},{6,3},{7,4},{8,5},{9,6},... | collective-permute-start | bytes 110600 | tf_op jit(solution)/shard_map/ppermute | solution.py:17
  41.3 4.4 fusion.1
  116.7 5.6 collective-permute-start.20
  125.2 7.2 %collective-permute-start = (f32[4,2,9,256]{3,2,1,0:T(8,128)S(1)}, f32[4,2,9,256]{3,2,1,0:T(8,128)S(1)}, u32[]{:S(2)}, u32[]{:S(2)}) collective-permute-start(f32[4,2,9,256]{3,2,1,0:T(8,128)S(1)} %copy-done.60), channel_id=1, source_target_pairs={{0,255},{1,0},{2,1},{3,2},{4,3},{5,4},{6,5},{7,6},{8,7},{9,8},{10,... | collective-permute-start | bytes 221192 | tf_op jit(solution)/shard_map/ppermute | solution.py:17
  147.4 7.8 %collective-permute-start.2 = (f32[4,2,9,256]{3,2,1,0:T(8,128)}, f32[4,2,9,256]{3,2,1,0:T(8,128)}, u32[]{:S(2)}, u32[]{:S(2)}) collective-permute-start(f32[4,2,9,256]{3,2,1,0:T(8,128)} %get-tuple-element.125), channel_id=1, source_target_pairs={{0,255},{1,0},{2,1},{3,2},{4,3},{5,4},{6,5},{7,6},{8,7},{9,8},{10,... | collective-permute-start | bytes 221192 | tf_op jit(solution)/shard_map/ppermute | solution.py:17
  159.4 4.8 reshape.518
  167.5 4.8 reshape.519
  179.2 4.1 tile.144
  183.4 3.5 tile.146
  186.9 4.8 tile.147
  201.8 7.6 %collective-permute-start.6 = (f32[4,9,256]{2,1,0:T(8,128)}, f32[4,9,256]{2,1,0:T(8,128)}, u32[]{:S(2)}, u32[]{:S(2)}) collective-permute-start(f32[4,9,256]{2,1,0:T(8,128)} %get-tuple-element.141), channel_id=1, source_target_pairs={{0,253},{1,254},{2,255},{3,0},{4,1},{5,2},{6,3},{7,4},{8,5},{9,6},... | collective-permute-start | bytes 110600 | tf_op jit(solution)/shard_map/ppermute | solution.py:17
  234.6 4.8 tile.165
  241.9 4.8 tile.167
  253.3 4.1 reshape.496
  260.8 4.1 reshape.492
  272.1 4.4 fusion
  284.6 5.3 collective-permute-start.10
  359.8 5.0 collective-permute-start.42
  369.8 3.6 multiply_add_fusion
  391.4 3.9 collective-permute-done.40
  406.8 9.3 %collective-permute-start.32 = (f32[4,9,256]{2,0,1:T(4,128)S(1)}, f32[4,9,256]{2,0,1:T(4,128)S(1)}, u32[]{:S(2)}, u32[]{:S(2)}) collective-permute-start(f32[4,9,256]{2,0,1:T(4,128)S(1)} %slice.620), channel_id=1, source_target_pairs={{0,253},{1,254},{2,255},{3,0},{4,1},{5,2},{6,3},{7,4},{8,5},{9,6},... | collective-permute-start | bytes 110600 | tf_op jit(solution)/shard_map/ppermute | solution.py:17
  425.9 4.8 reshape.521
  434.0 4.8 reshape.522
  463.7 4.8 collective-permute-start.12
  488.6 4.8 tile.156
  495.9 4.8 tile.159
  511.9 4.5 collective-permute-start.15
  525.5 4.8 tile.173
  533.7 4.8 tile.175
  558.6 4.8 reshape.515
  563.3 4.0 broadcast_in_dim.438
  567.3 4.8 reshape.511
  (698 shorter events, 413.1 us)
Async XLA Ops:
  3.8 121.4 %collective-permute-start.24 = (f32[4,9,256]{2,0,1:T(4,128)}, f32[4,9,256]{2,0,1:T(4,128)}, u32[]{:S(2)}, u32[]{:S(2)}) collective-permute-start(f32[4,9,256]{2,0,1:T(4,128)} %slice.601), channel_id=1, source_target_pairs={{0,253},{1,254},{2,255},{3,0},{4,1},{5,2},{6,3},{7,4},{8,5},{9,6},... | collective-permute-start | bytes 110600 | tf_op jit(solution)/shard_map/ppermute | solution.py:17
  15.4 109.8 %collective-permute-start.23 = (f32[4,9,256]{2,0,1:T(4,128)}, f32[4,9,256]{2,0,1:T(4,128)}, u32[]{:S(2)}, u32[]{:S(2)}) collective-permute-start(f32[4,9,256]{2,0,1:T(4,128)} %slice.601), channel_id=1, source_target_pairs={{0,254},{1,255},{2,0},{3,1},{4,2},{5,3},{6,4},{7,5},{8,6},{9,7},{1... | collective-permute-start | bytes 110600 | tf_op jit(solution)/shard_map/ppermute | solution.py:17
  19.0 95.9 %collective-permute-start.27 = (f32[4,9,256]{2,0,1:T(4,128)}, f32[4,9,256]{2,0,1:T(4,128)}, u32[]{:S(2)}, u32[]{:S(2)}) collective-permute-start(f32[4,9,256]{2,0,1:T(4,128)} %slice.602), channel_id=1, source_target_pairs={{0,3},{1,4},{2,5},{3,6},{4,7},{5,8},{6,9},{7,10},{8,11},{9,12},{10... | collective-permute-start | bytes 110600 | tf_op jit(solution)/shard_map/ppermute | solution.py:17
  20.8 94.6 %collective-permute-start.26 = (f32[4,9,256]{2,0,1:T(4,128)}, f32[4,9,256]{2,0,1:T(4,128)}, u32[]{:S(2)}, u32[]{:S(2)}) collective-permute-start(f32[4,9,256]{2,0,1:T(4,128)} %slice.602), channel_id=1, source_target_pairs={{0,2},{1,3},{2,4},{3,5},{4,6},{5,7},{6,8},{7,9},{8,10},{9,11},{10,... | collective-permute-start | bytes 110600 | tf_op jit(solution)/shard_map/ppermute | solution.py:17
  20.8 95.8 %collective-permute-start.25 = (f32[4,9,256]{2,0,1:T(4,128)}, f32[4,9,256]{2,0,1:T(4,128)}, u32[]{:S(2)}, u32[]{:S(2)}) collective-permute-start(f32[4,9,256]{2,0,1:T(4,128)} %slice.602), channel_id=1, source_target_pairs={{0,1},{1,2},{2,3},{3,4},{4,5},{5,6},{6,7},{7,8},{8,9},{9,10},{10,1... | collective-permute-start | bytes 110600 | tf_op jit(solution)/shard_map/ppermute | solution.py:17
  114.9 17.5 %collective-permute-start.22 = (f32[4,9,256]{2,0,1:T(4,128)}, f32[4,9,256]{2,0,1:T(4,128)S(1)}, u32[]{:S(2)}, u32[]{:S(2)}) collective-permute-start(f32[4,9,256]{2,0,1:T(4,128)} %slice.601), channel_id=1, source_target_pairs={{0,255},{1,0},{2,1},{3,2},{4,3},{5,4},{6,5},{7,6},{8,7},{9,8},{10,... | collective-permute-start | bytes 110600 | tf_op jit(solution)/shard_map/ppermute | solution.py:17
  115.4 94.6 %collective-permute-start.21 = (f32[4,4,9,256]{3,0,2,1:T(4,128)}, f32[4,4,9,256]{3,0,2,1:T(4,128)}, u32[]{:S(2)}, u32[]{:S(2)}) collective-permute-start(f32[4,4,9,256]{3,0,2,1:T(4,128)} %get-tuple-element.119), channel_id=1, source_target_pairs={{0,1},{1,2},{2,3},{3,4},{4,5},{5,6},{6,7},{7,8},{8,9},{9,10},{10,1... | collective-permute-start | bytes 442376 | tf_op jit(solution)/shard_map/ppermute | solution.py:17
  116.7 96.3 %collective-permute-start.20 = (f32[4,4,9,256]{3,0,2,1:T(4,128)}, f32[4,4,9,256]{3,0,2,1:T(4,128)}, u32[]{:S(2)}, u32[]{:S(2)}) collective-permute-start(f32[4,4,9,256]{3,0,2,1:T(4,128)} %get-tuple-element.119), channel_id=1, source_target_pairs={{0,255},{1,0},{2,1},{3,2},{4,3},{5,4},{6,5},{7,6},{8,7},{9,8},{10,... | collective-permute-start | bytes 442376 | tf_op jit(solution)/shard_map/ppermute | solution.py:17
  125.2 9.2 %collective-permute-start.1 = (f32[4,2,9,256]{3,2,1,0:T(8,128)S(1)}, f32[4,2,9,256]{3,2,1,0:T(8,128)S(1)}, u32[]{:S(2)}, u32[]{:S(2)}) collective-permute-start(f32[4,2,9,256]{3,2,1,0:T(8,128)S(1)} %copy-done.60), channel_id=1, source_target_pairs={{0,1},{1,2},{2,3},{3,4},{4,5},{5,6},{6,7},{7,8},{8,9},{9,10},{10,1... | collective-permute-start | bytes 221192 | tf_op jit(solution)/shard_map/ppermute | solution.py:17
  147.4 25.3 %collective-permute-start.3 = (f32[4,2,9,256]{3,2,1,0:T(8,128)}, f32[4,2,9,256]{3,2,1,0:T(8,128)}, u32[]{:S(2)}, u32[]{:S(2)}) collective-permute-start(f32[4,2,9,256]{3,2,1,0:T(8,128)} %get-tuple-element.125), channel_id=1, source_target_pairs={{0,1},{1,2},{2,3},{3,4},{4,5},{5,6},{6,7},{7,8},{8,9},{9,10},{10,1... | collective-permute-start | bytes 221192 | tf_op jit(solution)/shard_map/ppermute | solution.py:17
  147.4 25.3 %collective-permute-start.2 = (f32[4,2,9,256]{3,2,1,0:T(8,128)}, f32[4,2,9,256]{3,2,1,0:T(8,128)}, u32[]{:S(2)}, u32[]{:S(2)}) collective-permute-start(f32[4,2,9,256]{3,2,1,0:T(8,128)} %get-tuple-element.125), channel_id=1, source_target_pairs={{0,255},{1,0},{2,1},{3,2},{4,3},{5,4},{6,5},{7,6},{8,7},{9,8},{10,... | collective-permute-start | bytes 221192 | tf_op jit(solution)/shard_map/ppermute | solution.py:17
  201.8 44.9 %collective-permute-start.6 = (f32[4,9,256]{2,1,0:T(8,128)}, f32[4,9,256]{2,1,0:T(8,128)}, u32[]{:S(2)}, u32[]{:S(2)}) collective-permute-start(f32[4,9,256]{2,1,0:T(8,128)} %get-tuple-element.141), channel_id=1, source_target_pairs={{0,253},{1,254},{2,255},{3,0},{4,1},{5,2},{6,3},{7,4},{8,5},{9,6},... | collective-permute-start | bytes 110600 | tf_op jit(solution)/shard_map/ppermute | solution.py:17
  209.5 37.4 %collective-permute-start.5 = (f32[4,9,256]{2,1,0:T(8,128)}, f32[4,9,256]{2,1,0:T(8,128)}, u32[]{:S(2)}, u32[]{:S(2)}) collective-permute-start(f32[4,9,256]{2,1,0:T(8,128)} %get-tuple-element.141), channel_id=1, source_target_pairs={{0,254},{1,255},{2,0},{3,1},{4,2},{5,3},{6,4},{7,5},{8,6},{9,7},{1... | collective-permute-start | bytes 110600 | tf_op jit(solution)/shard_map/ppermute | solution.py:17
  209.7 37.2 %collective-permute-start.4 = (f32[4,9,256]{2,1,0:T(8,128)}, f32[4,9,256]{2,1,0:T(8,128)}, u32[]{:S(2)}, u32[]{:S(2)}) collective-permute-start(f32[4,9,256]{2,1,0:T(8,128)} %get-tuple-element.141), channel_id=1, source_target_pairs={{0,255},{1,0},{2,1},{3,2},{4,3},{5,4},{6,5},{7,6},{8,7},{9,8},{10,... | collective-permute-start | bytes 110600 | tf_op jit(solution)/shard_map/ppermute | solution.py:17
  210.0 38.5 %collective-permute-start.9 = (f32[4,9,256]{2,1,0:T(8,128)}, f32[4,9,256]{2,1,0:T(8,128)}, u32[]{:S(2)}, u32[]{:S(2)}) collective-permute-start(f32[4,9,256]{2,1,0:T(8,128)} %get-tuple-element.142), channel_id=1, source_target_pairs={{0,3},{1,4},{2,5},{3,6},{4,7},{5,8},{6,9},{7,10},{8,11},{9,12},{10... | collective-permute-start | bytes 110600 | tf_op jit(solution)/shard_map/ppermute | solution.py:17
  213.0 35.4 %collective-permute-start.8 = (f32[4,9,256]{2,1,0:T(8,128)}, f32[4,9,256]{2,1,0:T(8,128)}, u32[]{:S(2)}, u32[]{:S(2)}) collective-permute-start(f32[4,9,256]{2,1,0:T(8,128)} %get-tuple-element.142), channel_id=1, source_target_pairs={{0,2},{1,3},{2,4},{3,5},{4,6},{5,7},{6,8},{7,9},{8,10},{9,11},{10,... | collective-permute-start | bytes 110600 | tf_op jit(solution)/shard_map/ppermute | solution.py:17
  282.4 156.4 %collective-permute-start.11 = (f32[4,2,9,256]{3,2,0,1:T(8,128)}, f32[4,2,9,256]{3,2,0,1:T(8,128)}, u32[]{:S(2)}, u32[]{:S(2)}) collective-permute-start(f32[4,2,9,256]{3,2,0,1:T(8,128)} %get-tuple-element.123), channel_id=1, source_target_pairs={{0,1},{1,2},{2,3},{3,4},{4,5},{5,6},{6,7},{7,8},{8,9},{9,10},{10,1... | collective-permute-start | bytes 221192 | tf_op jit(solution)/shard_map/ppermute | solution.py:17
  284.6 154.2 %collective-permute-start.10 = (f32[4,2,9,256]{3,2,0,1:T(8,128)}, f32[4,2,9,256]{3,2,0,1:T(8,128)}, u32[]{:S(2)}, u32[]{:S(2)}) collective-permute-start(f32[4,2,9,256]{3,2,0,1:T(8,128)} %get-tuple-element.123), channel_id=1, source_target_pairs={{0,255},{1,0},{2,1},{3,2},{4,3},{5,4},{6,5},{7,6},{8,7},{9,8},{10,... | collective-permute-start | bytes 221192 | tf_op jit(solution)/shard_map/ppermute | solution.py:17
  357.8 28.7 %collective-permute-start.43 = (f32[4,9,64]{2,1,0:T(8,128)}, f32[4,9,64]{2,1,0:T(8,128)}, u32[]{:S(2)}, u32[]{:S(2)}) collective-permute-start(f32[4,9,64]{2,1,0:T(8,128)} %get-tuple-element.112), channel_id=1, source_target_pairs={{0,253},{1,254},{2,255},{3,0},{4,1},{5,2},{6,3},{7,4},{8,5},{9,6},... | collective-permute-start | bytes 27656 | tf_op jit(solution)/shard_map/ppermute | solution.py:17
  359.8 30.0 %collective-permute-start.42 = (f32[4,9,64]{2,1,0:T(8,128)}, f32[4,9,64]{2,1,0:T(8,128)}, u32[]{:S(2)}, u32[]{:S(2)}) collective-permute-start(f32[4,9,64]{2,1,0:T(8,128)} %get-tuple-element.112), channel_id=1, source_target_pairs={{0,254},{1,255},{2,0},{3,1},{4,2},{5,3},{6,4},{7,5},{8,6},{9,7},{1... | collective-permute-start | bytes 27656 | tf_op jit(solution)/shard_map/ppermute | solution.py:17
  364.8 25.8 %collective-permute-start.41 = (f32[4,9,64]{2,1,0:T(8,128)}, f32[4,9,64]{2,1,0:T(8,128)}, u32[]{:S(2)}, u32[]{:S(2)}) collective-permute-start(f32[4,9,64]{2,1,0:T(8,128)} %get-tuple-element.112), channel_id=1, source_target_pairs={{0,255},{1,0},{2,1},{3,2},{4,3},{5,4},{6,5},{7,6},{8,7},{9,8},{10,... | collective-permute-start | bytes 27656 | tf_op jit(solution)/shard_map/ppermute | solution.py:17
  399.3 16.8 %collective-permute-start.34 = (f32[4,9,256]{2,0,1:T(4,128)S(1)}, f32[4,9,256]{2,0,1:T(4,128)S(1)}, u32[]{:S(2)}, u32[]{:S(2)}) collective-permute-start(f32[4,9,256]{2,0,1:T(4,128)S(1)} %slice.621), channel_id=1, source_target_pairs={{0,2},{1,3},{2,4},{3,5},{4,6},{5,7},{6,8},{7,9},{8,10},{9,11},{10,... | collective-permute-start | bytes 110600 | tf_op jit(solution)/shard_map/ppermute | solution.py:17
  402.7 13.5 %collective-permute-start.33 = (f32[4,9,256]{2,0,1:T(4,128)S(1)}, f32[4,9,256]{2,0,1:T(4,128)S(1)}, u32[]{:S(2)}, u32[]{:S(2)}) collective-permute-start(f32[4,9,256]{2,0,1:T(4,128)S(1)} %slice.621), channel_id=1, source_target_pairs={{0,1},{1,2},{2,3},{3,4},{4,5},{5,6},{6,7},{7,8},{8,9},{9,10},{10,1... | collective-permute-start | bytes 110600 | tf_op jit(solution)/shard_map/ppermute | solution.py:17
  406.8 11.6 %collective-permute-start.32 = (f32[4,9,256]{2,0,1:T(4,128)S(1)}, f32[4,9,256]{2,0,1:T(4,128)S(1)}, u32[]{:S(2)}, u32[]{:S(2)}) collective-permute-start(f32[4,9,256]{2,0,1:T(4,128)S(1)} %slice.620), channel_id=1, source_target_pairs={{0,253},{1,254},{2,255},{3,0},{4,1},{5,2},{6,3},{7,4},{8,5},{9,6},... | collective-permute-start | bytes 110600 | tf_op jit(solution)/shard_map/ppermute | solution.py:17
  418.4 51.2 %collective-permute-start.29 = (f32[4,4,9,256]{3,0,2,1:T(4,128)}, f32[4,4,9,256]{3,0,2,1:T(4,128)}, u32[]{:S(2)}, u32[]{:S(2)}) collective-permute-start(f32[4,4,9,256]{3,0,2,1:T(4,128)} %get-tuple-element.117), channel_id=1, source_target_pairs={{0,1},{1,2},{2,3},{3,4},{4,5},{5,6},{6,7},{7,8},{8,9},{9,10},{10,1... | collective-permute-start | bytes 442376 | tf_op jit(solution)/shard_map/ppermute | solution.py:17
  420.0 49.6 %collective-permute-start.28 = (f32[4,4,9,256]{3,0,2,1:T(4,128)}, f32[4,4,9,256]{3,0,2,1:T(4,128)}, u32[]{:S(2)}, u32[]{:S(2)}) collective-permute-start(f32[4,4,9,256]{3,0,2,1:T(4,128)} %get-tuple-element.117), channel_id=1, source_target_pairs={{0,255},{1,0},{2,1},{3,2},{4,3},{5,4},{6,5},{7,6},{8,7},{9,8},{10,... | collective-permute-start | bytes 442376 | tf_op jit(solution)/shard_map/ppermute | solution.py:17
  463.4 19.8 %collective-permute-start.13 = (f32[4,2,9,256]{3,2,1,0:T(8,128)}, f32[4,2,9,256]{3,2,1,0:T(8,128)}, u32[]{:S(2)}, u32[]{:S(2)}) collective-permute-start(f32[4,2,9,256]{3,2,1,0:T(8,128)} %get-tuple-element.121), channel_id=1, source_target_pairs={{0,1},{1,2},{2,3},{3,4},{4,5},{5,6},{6,7},{7,8},{8,9},{9,10},{10,1... | collective-permute-start | bytes 221192 | tf_op jit(solution)/shard_map/ppermute | solution.py:17
  463.7 19.6 %collective-permute-start.12 = (f32[4,2,9,256]{3,2,1,0:T(8,128)}, f32[4,2,9,256]{3,2,1,0:T(8,128)}, u32[]{:S(2)}, u32[]{:S(2)}) collective-permute-start(f32[4,2,9,256]{3,2,1,0:T(8,128)} %get-tuple-element.121), channel_id=1, source_target_pairs={{0,255},{1,0},{2,1},{3,2},{4,3},{5,4},{6,5},{7,6},{8,7},{9,8},{10,... | collective-permute-start | bytes 221192 | tf_op jit(solution)/shard_map/ppermute | solution.py:17
  509.6 35.4 %collective-permute-start.16 = (f32[4,9,256]{2,1,0:T(8,128)}, f32[4,9,256]{2,1,0:T(8,128)}, u32[]{:S(2)}, u32[]{:S(2)}) collective-permute-start(f32[4,9,256]{2,1,0:T(8,128)} %get-tuple-element.135), channel_id=1, source_target_pairs={{0,253},{1,254},{2,255},{3,0},{4,1},{5,2},{6,3},{7,4},{8,5},{9,6},... | collective-permute-start | bytes 110600 | tf_op jit(solution)/shard_map/ppermute | solution.py:17
  511.9 33.3 %collective-permute-start.15 = (f32[4,9,256]{2,1,0:T(8,128)}, f32[4,9,256]{2,1,0:T(8,128)}, u32[]{:S(2)}, u32[]{:S(2)}) collective-permute-start(f32[4,9,256]{2,1,0:T(8,128)} %get-tuple-element.135), channel_id=1, source_target_pairs={{0,254},{1,255},{2,0},{3,1},{4,2},{5,3},{6,4},{7,5},{8,6},{9,7},{1... | collective-permute-start | bytes 110600 | tf_op jit(solution)/shard_map/ppermute | solution.py:17
  516.4 28.8 %collective-permute-start.14 = (f32[4,9,256]{2,1,0:T(8,128)}, f32[4,9,256]{2,1,0:T(8,128)}, u32[]{:S(2)}, u32[]{:S(2)}) collective-permute-start(f32[4,9,256]{2,1,0:T(8,128)} %get-tuple-element.135), channel_id=1, source_target_pairs={{0,255},{1,0},{2,1},{3,2},{4,3},{5,4},{6,5},{7,6},{8,7},{9,8},{10,... | collective-permute-start | bytes 110600 | tf_op jit(solution)/shard_map/ppermute | solution.py:17
  538.5 11.9 %collective-permute-start.19 = (f32[4,9,256]{2,1,0:T(8,128)}, f32[4,9,256]{2,1,0:T(8,128)}, u32[]{:S(2)}, u32[]{:S(2)}) collective-permute-start(f32[4,9,256]{2,1,0:T(8,128)} %get-tuple-element.136), channel_id=1, source_target_pairs={{0,3},{1,4},{2,5},{3,6},{4,7},{5,8},{6,9},{7,10},{8,11},{9,12},{10... | collective-permute-start | bytes 110600 | tf_op jit(solution)/shard_map/ppermute | solution.py:17
  (119 other events, 851.9 us)
where the time goes:
time: 595 us; the launch traced here: 584 us
  local copies, waits for them, and re-layouts  357 us (60%)
  starting transfers between devices  101 us (17%)
  other arithmetic  90.3 us (15%)
  matrix products  22.8 us (4%)
  waiting for transfers between devices  9.32 us (2%)
    ppermute x44, starting transfers between devices, shifted_2(): lax.ppermute(shard, axis, [(i, (i + by) % devices) for i in range(devices)])  101 us
    another operation x20, local copies, waits for them, and re-layouts, spread_face(): tiled = jnp.tile(square_face, (1,) * (len(lead) + 1) + (extent,))  62.4 us
    slice x20, local copies, waits for them, and re-layouts, layer_of(): lax.slice_in_dim(flat, index, flat.shape[-1], stride=extent, axis=last_axis)  39.2 us
    reshape x8, local copies, waits for them, and re-layouts, spread_face(): return jnp.repeat(face, extent, axis=len(lead))  37 us
    broadcast_in_dim x8, local copies, waits for them, and re-layouts, spread_face(): return jnp.repeat(face, extent, axis=len(lead))  27 us
    gather x20, local copies, waits for them, and re-layouts, side_values(): nearby[distance[:, facing] + base, positions[:, facing], facing ^ 1]  22.2 us
    another operation x23, other arithmetic, collect(): return jnp.stack(pieces, axis=0)  18.2 us
    slice x20, local copies, waits for them, and re-layouts, layer_of(): lax.slice_in_dim(shaped, index * extent, (index + 1) * extent, axis=last_...  18 us
  transfers between devices with their start and end apart: 44, of which 7 were waited for; matrix products, arithmetic and copies ran while one was open for 64% of the time, Pallas kernels for 0%

commit v1 on v0

v1 whole, which is shorter than its diff:
```python
import jax
import jax.numpy as jnp
import numpy as np
from jax import lax
from jax.experimental import pallas as pl
from jax.experimental.pallas import tpu as pltpu
from jax.sharding import PartitionSpec as P

F32 = jnp.float32
VEL = [(a, b, c) for a in (-1, 0, 1) for b in (-1, 0, 1) for c in (-1, 0, 1)]
ROWS, LANES = 32, 128
CHUNK = 8


def shape_of(*dims):
    return jax.ShapeDtypeStruct(dims, F32)


def iota(rows, axis):
    return lax.broadcasted_iota(jnp.int32, (rows, LANES), axis)


def chunk_at(v):
    return pl.ds(pl.multiple_of(v * CHUNK, CHUNK), CHUNK)


def roll_lanes(x, by):
    if isinstance(by, int):
        by = by % LANES
        if by == 0:
            return x
    return pltpu.roll(x, by, 1)


def forward_moments(values):
    out = list(values)
    for stride in (9, 3, 1):
        for i in range(27):
            if (i // stride) % 3 == 0:
                low, mid, high = out[i], out[i + stride], out[i + 2 * stride]
                both = low + high
                out[i] = both + 4.0 * mid
                out[i + stride] = high - low
                out[i + 2 * stride] = both
    return out


def plus(x, y):
    if x is None:
        return y
    return x if y is None else x + y


def minus(x, y):
    if y is None:
        return x
    return -y if x is None else x - y


def backward_moments(values):
    out = list(values)
    for stride in (9, 3, 1):
        for i in range(27):
            if (i // stride) % 3 == 0:
                m0, m1, m2 = out[i], out[i + stride], out[i + 2 * stride]
                out[i] = minus(m2, m1)
                out[i + stride] = minus(m0, m2)
                out[i + 2 * stride] = plus(m1, m2)
    return out


def collide(g, rate):
    m = forward_moments(g)
    rho = m[0]
    j = (m[9], m[3], m[1])
    square = [x * x * (1.0 / 72.0) for x in j]
    relaxed = [None] * 27
    for k in range(27):
        digits = (k // 9, (k // 3) % 3, k % 3)
        odd = [d for d in range(3) if digits[d] == 1]
        twos = [d for d in range(3) if digits[d] == 2]
        if k in (0, 9, 3, 1):
            continue
        if not odd:
            level = rho
            for d in twos:
                level = level + square[d]
        elif len(odd) == 1:
            level = j[odd[0]]
        elif len(odd) == 2:
            level = j[odd[0]] * j[odd[1]] * (1.0 / 216.0)
        else:
            level = None
        if level is not None and twos:
            level = level * (3.0 ** -len(twos))
        relaxed[k] = minus(m[k], level) * (rate(k) * (1.0 / 64.0))
    back = backward_moments(relaxed)
    post = []
    for i, c in enumerate(VEL):
        factor = 2.0 ** sum(abs(x) for x in c)
        post.append(g[i] - (back[i] if factor == 1.0 else factor * back[i]))
    return post, j


def grow_index():
    r, l = iota(CHUNK, 0), iota(CHUNK, 1)
    return (r // 4) % 2 * 64 + r % 2 * 32 + l // 32 * 8 + l % 16 // 2


def grow_row(row, index):
    return jnp.take_along_axis(jnp.broadcast_to(row, (CHUNK, LANES)), index, axis=1)


PER_BLOCK = 36
FIELDS = 4 * PER_BLOCK + 1


def begin_kernel(
    info, levels_in, near_in, rates_in, pop, scal, old, new, out,
    pops, scals, olds, news, levels, near, rates, sems,
):
    layer, core = info[0], info[1]
    small = [
        pltpu.make_async_copy(a, b, sems.at[7 + i])
        for i, (a, b) in enumerate(((levels_in, levels), (near_in, near), (rates_in, rates)))
    ]
    for copy in small:
        copy.start()
    copies = []
    for v in range(4):
        rows = pl.ds(32 * v, 32)
        copies.append(pltpu.make_async_copy(pop.at[:, rows, :], pops.at[:, rows, :], sems.at[v]))
    copies.append(pltpu.make_async_copy(old, olds, sems.at[4]))
    copies.append(pltpu.make_async_copy(new, news, sems.at[5]))
    copies.append(pltpu.make_async_copy(scal, scals, sems.at[6]))
    for copy in copies:
        copy.start()
    index = grow_index()
    for copy in small:
        copy.wait()
    row, lane = iota(CHUNK, 0), iota(CHUNK, 1)
    meta = jnp.zeros((CHUNK, LANES), F32)
    for b in range(4):
        for q in range(6):
            here = jnp.logical_and(row == b, lane == q)
            meta = jnp.where(here, near[b, q].astype(F32), meta)
    out[FIELDS - 1, 0:8, :] = meta

    def fine_of(b):
        return levels[layer * 8 + core * 4 + b] == 1

    for v in range(4):
        copies[v].wait()

        @pl.loop(0, 4)
        def _(b):
            @pl.when(fine_of(b))
            def _():
                at = pl.ds(8 * v, 8)
                from_rows = pl.ds(32 * v + b, 8, stride=4)
                post, _j = collide([pops[p, from_rows, :] for p in range(27)], lambda k: rates[k])
                for p in range(27):
                    out[b * PER_BLOCK + p, at, :] = post[p]

    for copy in copies[4:]:
        copy.wait()

    @pl.loop(0, 4)
    def _(b):
        @pl.when(fine_of(b))
        def _():
            for m in range(9):
                for v in range(4):
                    out[b * PER_BLOCK + 27 + m, pl.ds(8 * v, 8), :] = scals[m, pl.ds(32 * v + b, 8, stride=4), :]

        @pl.when(jnp.logical_not(fine_of(b)))
        def _():
            for p in range(27):
                for v in range(4):
                    before = olds[p, pl.ds(4 * v + b, 1), :]
                    after = news[p, pl.ds(4 * v + b, 1), :]
                    out[b * PER_BLOCK + 27 + p // 8, pl.ds(p % 8 * 4 + v, 1), :] = 0.5 * (before + after)
                    out[b * PER_BLOCK + p, pl.ds(8 * v, 8), :] = grow_row(before, index)


def spot(block, core):
    return (block % 8) ^ (core * 4)


def y_up(own, beside, even, group):
    turned = jnp.where(even, pltpu.roll(beside, CHUNK - 1, 0), pltpu.roll(own, 1, 0))
    return roll_lanes(jnp.where(group < 7, own, turned), 16)


def y_down(own, beside, even, group):
    turned = jnp.where(even, pltpu.roll(own, CHUNK - 1, 0), pltpu.roll(beside, 1, 0))
    return roll_lanes(jnp.where(group > 0, own, turned), -16)


def chunks(ref, *lead):
    return [ref[(*lead, pl.ds(8 * v, 8), slice(None))] for v in range(4)]


def x_up(own, beyond, row):
    turned = [pltpu.roll(x, 2, 0) for x in own]
    before = [beyond] + turned[:3]
    return [jnp.where(row < 2, a, b) for a, b in zip(before, turned)]


def x_down(own, beyond, row):
    turned = [pltpu.roll(x, CHUNK - 2, 0) for x in own]
    after = turned[1:] + [beyond]
    return [jnp.where(row >= 6, a, b) for a, b in zip(after, turned)]


def put(ref, lead, values):
    for v in range(4):
        ref[(*lead, pl.ds(8 * v, 8), slice(None))] = values[v]


def sections_xy(halves, faces, mid, dest, near, core, fine_of):
    row = iota(CHUNK, 0)
    even = row % 2 == 0
    group = iota(CHUNK, 1) // 16

    for half, field in enumerate(halves):

        @pl.loop(0, 4)
        def _(i):
            for p, c in enumerate(VEL):
                ref, lead = field(i, p)
                if c[0] == 1:
                    faces[half * 4 + i, p] = pltpu.roll(ref[(*lead, pl.ds(24, 8), slice(None))], 2, 0)
                elif c[0] == -1:
                    faces[half * 4 + i, p] = pltpu.roll(ref[(*lead, pl.ds(0, 8), slice(None))], CHUNK - 2, 0)

    for half, field in enumerate(halves):

        @pl.loop(0, 4)
        def _(i):
            b = half * 4 + i
            fine = fine_of(b)

            @pl.when(fine)
            def _():
                low, high = spot(near[b, 0], core), spot(near[b, 1], core)
                for p, c in enumerate(VEL):
                    ref, lead = field(i, p)
                    values = chunks(ref, *lead)
                    if c[0] == 1:
                        values = x_up(values, faces[low, p], row)
                    elif c[0] == -1:
                        values = x_down(values, faces[high, p], row)
                    put(mid, (b, p), values)

            @pl.when(jnp.logical_not(fine))
            def _():
                for p in range(27):
                    ref, lead = field(i, p)
                    put(mid, (b, p), chunks(ref, *lead))

    @pl.loop(0, 8)
    def _(b):
        fine = fine_of(b)

        @pl.when(fine)
        def _():
            low, high = spot(near[b, 2], core), spot(near[b, 3], core)
            for p, c in enumerate(VEL):
                for v in range(4):
                    at = pl.ds(8 * v, 8)
                    value = mid[b, p, at, :]
                    if c[1] == 1:
                        value = y_up(value, mid[low, p, at, :], even, group)
                    elif c[1] == -1:
                        value = y_down(value, mid[high, p, at, :], even, group)
                    dest[b, p, at, :] = value

        @pl.when(jnp.logical_not(fine))
        def _():
            for p in range(27):
                if VEL[p][2] != 0:
                    put(dest, (b, p), chunks(mid, b, p))


def pack_into(fields, first_slot, start, lane):
    out = None
    for e, field in enumerate(fields):
        slot = first_slot + e
        moved = roll_lanes(field, slot - start)
        out = moved if out is None else jnp.where(lane == slot, moved, out)
    return out


def halves_of(own, other):
    return [lambda i, p: (own, (i * PER_BLOCK + p,)), lambda i, p: (other, (i * PER_BLOCK + p,))]


def plane_kernel(info, levels, near, own, other, dest, up, down, table, mid, faces, meta, sem):
    layer, core = info[0], info[1]
    copy = pltpu.make_async_copy(other.at[FIELDS - 1, pl.ds(0, 8), :], meta, sem)
    copy.start()
    copy.wait()
    for i in range(4):
        for q in range(6):
            table[i, q] = near[i, q]
            table[4 + i, q] = meta[i, q].astype(jnp.int32)

    def fine_of(b):
        return levels[layer * 8 + spot(b, core)] == 1

    sections_xy(halves_of(own, other), faces, mid, dest, table, core, fine_of)
    lane = iota(CHUNK, 1) % 16

    for half, ref_in in enumerate((own, other)):

        @pl.loop(0, 4)
        def _(i):
            b = half * 4 + i
            for v in range(4):
                at = pl.ds(8 * v, 8)
                for ref, digit, start in ((up, 2, 15), (down, 0, 0)):
                    fields = [dest[b, 3 * e + digit, at, :] for e in range(9)]
                    fields += [ref_in[i * PER_BLOCK + 27 + e, at, :] for e in range(7)]
                    ref[b, at, :] = pack_into(fields, 0, start, lane)
                    held = ref[8, at, :]
                    for e in range(2):
                        slot = 2 * b + e
                        moved = pltpu.roll(ref_in[i * PER_BLOCK + 34 + e, at, :], (slot - start) % LANES, 1)
                        held = jnp.where(lane == slot, moved, held)
                    ref[8, at, :] = held


def z_section(h, up, down, depth):
    g = []
    for p, c in enumerate(VEL):
        e = p // 3
        value = h(p)
        if c[2] == 1:
            value = jnp.where(depth == 0, roll_lanes(up, -e), roll_lanes(value, 1))
        elif c[2] == -1:
            value = jnp.where(depth == 15, roll_lanes(down, 15 - e), roll_lanes(value, -1))
        g.append(value)
    return g


def species_step(y_ref, b, sides, faces, flux, flags, diffusivity, stoichiometry, store):
    row, lanes = iota(CHUNK, 0), iota(CHUNK, 1)
    even = row % 2 == 0
    group, depth = lanes // 16, lanes % 16

    def gone(edge, q):
        return jnp.logical_and(edge, flags[q] != 1)

    lost = [
        gone(row < 2, 0), gone(row >= 6, 1),
        gone(jnp.logical_and(even, group == 0), 2), gone(jnp.logical_and(jnp.logical_not(even), group == 7), 3),
        gone(depth == 0, 4), gone(depth == 15, 5),
    ]
    burning = [
        a * c * jnp.exp(4.0 * (t - 1.0))
        for a, c, t in zip(chunks(y_ref, b, 0), chunks(y_ref, b, 1), chunks(y_ref, b, 8))
    ]
    for m in range(9):
        y = chunks(y_ref, b, m)
        low_x = pltpu.roll(y_ref[sides[0], m, pl.ds(24, 8), :], 2, 0)
        high_x = pltpu.roll(y_ref[sides[1], m, pl.ds(0, 8), :], CHUNK - 2, 0)
        lower_x, upper_x = x_up(y, low_x, row), x_down(y, high_x, row)
        lower_x[0] = jnp.where(lost[0], y[0], lower_x[0])
        upper_x[3] = jnp.where(lost[1], y[3], upper_x[3])
        for v in range(4):
            at = pl.ds(8 * v, 8)
            here = y[v]
            z_low, z_high = faces(m, at)
            pairs = [
                (lower_x[v], upper_x[v]),
                (
                    jnp.where(lost[2], here, y_up(here, y_ref[sides[2], m, at, :], even, group)),
                    jnp.where(lost[3], here, y_down(here, y_ref[sides[3], m, at, :], even, group)),
                ),
                (
                    jnp.where(lost[4], here, jnp.where(depth == 0, z_low, roll_lanes(here, 1))),
                    jnp.where(lost[5], here, jnp.where(depth == 15, z_high, roll_lanes(here, -1))),
                ),
            ]
            drift = spread = None
            for d, (lower, upper) in enumerate(pairs):
                part = flux[d, at, :] * (upper - lower)
                both = upper + lower
                drift = part if drift is None else drift + part
                spread = both if spread is None else spread + both
            value = here - drift + diffusivity[m] * (spread - 6.0 * here) + stoichiometry[m] * burning[v]
            store(m, v, value)


WIDE = 640


def reduce_tables():
    l = np.arange(LANES)[:, None]
    c = np.arange(WIDE)[None, :]
    e, cell = c // 64, c % 64
    live = c < 576
    along_x = (l // 32 * 8 + l % 16 // 2 == cell % 32) & live
    along_y = [(l // 16 + 8 * a == e) & (l % 16 // 2 == cell % 8) & live for a in range(2)]
    along_z = (l % 16 == e) & (l // 32 == cell % 4) & live
    side = np.concatenate([along_x, along_y[0], along_y[1]], axis=0)
    return jnp.asarray(side, F32), jnp.asarray(along_z, F32)


def wide_iota(axis):
    return lax.broadcasted_iota(jnp.int32, (ROWS, WIDE), axis)


def times(x, w):
    return jnp.dot(x, w, precision=lax.Precision.HIGHEST, preferred_element_type=F32)


def put_pair(out, s, base, first, second):
    moved = pltpu.roll(second, 64, 1)
    out[pl.ds(s, 1), pl.ds(base, 512)] = first[:, 0:512]
    out[pl.ds(s, 1), pl.ds(base + 512, 128)] = first[:, 512:640] + moved[:, 0:128]
    out[pl.ds(s, 1), pl.ds(base + 640, 512)] = moved[:, 128:640]


def middle_kernel(
    info, levels, near, rates, diffusivity, stoichiometry, own, other, held, up_in, down_in, tables,
    flow, species, up, down, sides_out,
    first, mid, old, faces, flux, edge_x, edge_y, inverse,
):
    layer, core = info[0], info[1]
    index = grow_index()
    depth = iota(CHUNK, 1) % 16

    def fine_of(b):
        return levels[layer * 8 + spot(b, core)] == 1

    @pl.loop(0, 8)
    def _(b):
        inverse[0, spot(near[b, 5], core)] = b
        inverse[1, spot(near[b, 4], core)] = b

    for half, ref_in in enumerate((own, other)):

        @pl.loop(0, 4)
        def _(i):
            for m in range(9):
                put(old, (half * 4 + i, m), chunks(ref_in, i * PER_BLOCK + 27 + m))

            @pl.when(jnp.logical_not(fine_of(half * 4 + i)))
            def _():
                for p in range(27):
                    for v in range(4):
                        line = ref_in[i * PER_BLOCK + 27 + p // 8, pl.ds(p % 8 * 4 + v, 1), :]
                        first[half * 4 + i, p, pl.ds(8 * v, 8), :] = grow_row(line, index)

    @pl.loop(0, 8)
    def _(b):
        @pl.when(fine_of(b))
        def _():
            below, above = spot(near[b, 4], core), spot(near[b, 5], core)

            @pl.loop(0, 4)
            def _(v):
                at = chunk_at(v)
                g = z_section(lambda p: held[b, p, at, :], up_in[below, at, :], down_in[above, at, :], depth)
                post, j = collide(g, lambda k: rates[k])
                for p in range(27):
                    first[b, p, at, :] = post[p]
                for d in range(3):
                    flux[d, at, :] = j[d] * (0.5 / 216.0)

            def z_faces(m, at):
                if m < 7:
                    slot = 9 + m
                    return roll_lanes(up_in[below, at, :], -slot), roll_lanes(down_in[above, at, :], 15 - slot)
                low = LANES - 2 * below - (m - 7)
                high = (LANES + 15 - 2 * above - (m - 7)) % LANES
                return pltpu.roll(up_in[8, at, :], low, 1), pltpu.roll(down_in[8, at, :], high, 1)

            def store(m, v, value):
                species[b, m, pl.ds(8 * v, 8), :] = value

            species_step(
                old, b, [spot(near[b, q], core) for q in range(4)], z_faces, flux,
                [levels[near[b, q]] for q in range(6)], diffusivity, stoichiometry, store,
            )

        @pl.when(jnp.logical_not(fine_of(b)))
        def _():
            species[b] = jnp.zeros((9, ROWS, LANES), F32)

    sections_xy([lambda i, p: (first, (i, p)), lambda i, p: (first, (4 + i, p))], faces, mid, flow, near, core, fine_of)

    for way, (ref, digit, start) in enumerate(((up, 2, 15), (down, 0, 0))):
        for half, ref_in in enumerate((own, other)):

            @pl.loop(0, 4)
            def _(i):
                b = half * 4 + i
                target = spot(near[b, 5 - way], core)

                @pl.when(target < 4)
                def _():
                    for v in range(4):
                        at = pl.ds(8 * v, 8)
                        fields = [flow[b, 3 * e + digit, at, :] for e in range(9)]
                        fields += [species[b, e, at, :] for e in range(7)]
                        ref[2 * target, at, :] = pack_into(fields, 0, start, depth)
                        fields = [
                            0.125 * (ref_in[i * PER_BLOCK + 3 * e + digit, at, :] + first[b, 3 * e + digit, at, :])
                            for e in range(9)
                        ]
                        fields += [species[b, 7, at, :], species[b, 8, at, :]]
                        ref[2 * target + 1, at, :] = pack_into(fields, 0, start, depth)

    group, odd = iota(CHUNK, 1) // 16, iota(CHUNK, 0) % 2 == 1
    for half, ref_in in enumerate((own, other)):

        @pl.loop(0, 4)
        def _(i):
            b = half * 4 + i

            @pl.when(fine_of(b))
            def _():
                for side in range(2):
                    at = pl.ds(30, 2) if side == 0 else pl.ds(0, 2)
                    for e in range(9):
                        p = 18 + e if side == 0 else e
                        edge_x[b, side, pl.ds(2 * e, 2), :] = ref_in[i * PER_BLOCK + p, at, :] + first[b, p, at, :]
                    edge_x[b, side, pl.ds(18, 14), :] = jnp.zeros((14, LANES), F32)
                for v in range(4):
                    at = pl.ds(8 * v, 8)
                    packs = [None, None]
                    for e in range(9):
                        p_low = 9 * (e // 3) + e % 3
                        p_high = p_low + 6
                        high = ref_in[i * PER_BLOCK + p_high, at, :] + first[b, p_high, at, :]
                        low = ref_in[i * PER_BLOCK + p_low, at, :] + first[b, p_low, at, :]
                        slot = e % 8
                        both = jnp.where(odd, roll_lanes(high, 16 * (slot - 7)), roll_lanes(low, 16 * slot))
                        held_pack = packs[e // 8]
                        packs[e // 8] = both if held_pack is None else jnp.where(group == slot, both, held_pack)
                    for a in range(2):
                        edge_y[b, a, at, :] = packs[a]

    row, col = wide_iota(0), wide_iota(1)
    e_of, cell = col // 64, col % 64
    keep_x = jnp.logical_and(row // 2 == e_of, row % 2 == cell // 32)
    keep_y = row // 4 == cell // 8
    odd_row = row % 2 == 1

    for s in range(4):
        coarse = jnp.logical_not(fine_of(s))

        @pl.when(coarse)
        def _(s=s):
            weight = [jnp.where(levels[near[s, q]] == 1, 0.125, 0.0) for q in range(4)]
            at = [spot(near[s, q], core) for q in range(4)]
            rows = []
            for q in range(2):
                face = jnp.where(levels[near[s, q]] == 1, edge_x[at[q], q], 0.0)
                spread = times(face, tables[0:128, :])
                rows.append(weight[q] * jnp.sum(jnp.where(keep_x, spread, 0.0), axis=0, keepdims=True))
            put_pair(sides_out, s, 0, rows[0], rows[1])
            rows = []
            for q in (2, 3):
                fine = levels[near[s, q]] == 1
                spread = times(jnp.where(fine, edge_y[at[q], 0], 0.0), tables[128:256, :])
                spread += times(jnp.where(fine, edge_y[at[q], 1], 0.0), tables[256:384, :])
                keep = jnp.logical_and(keep_y, odd_row if q == 2 else jnp.logical_not(odd_row))
                rows.append(weight[q] * jnp.sum(jnp.where(keep, spread, 0.0), axis=0, keepdims=True))
            put_pair(sides_out, s, 1152, rows[0], rows[1])

        @pl.when(jnp.logical_not(coarse))
        def _(s=s):
            sides_out[pl.ds(s, 1), :] = jnp.zeros((1, 2304), F32)


def end_kernel(
    info, levels, near, diffusivity, stoichiometry, held, species, up_in, down_in, sides, table, pop, scal,
    pop_out, scal_out, returned,
    pops, scals, flux, sems,
):
    layer, core = info[0], info[1]
    depth = iota(CHUNK, 1) % 16
    row, col = wide_iota(0), wide_iota(1)
    keep = row // 4 * 2 + row % 2 == col % 64 // 4

    def fine_of(s):
        return levels[layer * 8 + core * 4 + s] == 1

    copies = []
    for v in range(4):
        at = pl.ds(8 * v, 8)

        @pl.loop(0, 4)
        def _(s):
            rows = pl.ds(32 * v + s, 8, stride=4)

            @pl.when(fine_of(s))
            def _():
                g = z_section(lambda p: held[s, p, at, :], up_in[2 * s, at, :], down_in[2 * s, at, :], depth)
                for p in range(27):
                    pops[p, rows, :] = g[p]
                m = forward_moments(g)
                for d, i in enumerate((9, 3, 1)):
                    flux[s, d, at, :] = m[i] * (0.5 / 216.0)

            @pl.when(jnp.logical_not(fine_of(s)))
            def _():
                for p in range(27):
                    pops[p, rows, :] = pop[p, rows, :]

        rows = pl.ds(32 * v, 32)
        copies.append(pltpu.make_async_copy(pops.at[:, rows, :], pop_out.at[:, rows, :], sems.at[v]))
        copies[-1].start()

    @pl.loop(0, 4)
    def _(s):
        @pl.when(fine_of(s))
        def _():
            def z_faces(m, at):
                a, slot = (2 * s, 9 + m) if m < 7 else (2 * s + 1, 2 + m)
                return roll_lanes(up_in[a, at, :], -slot), roll_lanes(down_in[a, at, :], 15 - slot)

            def store(m, v, value):
                scals[m, pl.ds(32 * v + s, 8, stride=4), :] = value

            species_step(
                species, s, [spot(near[s, q], core) for q in range(4)], z_faces, flux.at[s],
                [levels[near[s, q]] for q in range(6)], diffusivity, stoichiometry, store,
            )

        @pl.when(jnp.logical_not(fine_of(s)))
        def _():
            for v in range(4):
                at = pl.ds(32 * v + s, 8, stride=4)
                for m in range(9):
                    scals[m, at, :] = scal[m, at, :]

    copies.append(pltpu.make_async_copy(scals, scal_out, sems.at[4]))
    copies[-1].start()
    returned[:, 0:2304] = sides[...]
    for s in range(4):
        coarse = levels[layer * 8 + core * 4 + s] != 1

        @pl.when(coarse)
        def _(s=s):
            rows = []
            for a, ref in enumerate((up_in, down_in)):
                face = jnp.where(levels[near[s, 4 + a]] == 1, ref[2 * s + 1], 0.0)
                rows.append(jnp.sum(jnp.where(keep, times(face, table[...]), 0.0), axis=0, keepdims=True))
            put_pair(returned, s, 2304, rows[0], rows[1])

        @pl.when(jnp.logical_not(coarse))
        def _(s=s):
            returned[pl.ds(s, 1), pl.ds(2304, 1152)] = jnp.zeros((1, 1152), F32)

    for copy in copies:
        copy.wait()


def specs(kinds):
    table = {
        "s": pl.BlockSpec(memory_space=pltpu.SMEM),
        "v": pl.BlockSpec(memory_space=pltpu.VMEM),
        "h": pl.BlockSpec(memory_space=pltpu.HBM),
    }
    return [table[kind] for kind in kinds]


def call(kernel, kinds, outs, out_kinds, scratch, name, megabytes, flops):
    return pl.pallas_call(
        kernel,
        in_specs=specs(kinds),
        out_specs=specs(out_kinds),
        out_shape=outs,
        scratch_shapes=scratch,
        name=name,
        compiler_params=pltpu.CompilerParams(vmem_limit_bytes=megabytes << 20),
        cost_estimate=pl.CostEstimate(flops=flops, transcendentals=0, bytes_accessed=8 << 20),
    )


def interleave(x):
    blocks, n, cells = x.shape
    x = x.reshape(blocks, n, cells // LANES, LANES)
    return jnp.transpose(x, (1, 2, 0, 3)).reshape(n, cells // LANES * blocks, LANES)


def separate(x):
    n, rows, _ = x.shape
    x = jnp.transpose(x.reshape(n, rows // 4, 4, LANES), (2, 0, 1, 3))
    return x.reshape(4, n, rows // 4 * LANES)


def local(
    populations, scalars, coarse_old, coarse_new, levels, neighbours, relax_rates, diffusivity, stoichiometry
):
    devices = lax.axis_size("blk")
    me = lax.axis_index("blk")
    info = jnp.stack([me // 2, me % 2]).astype(jnp.int32)
    swap = [(i, i ^ 1) for i in range(devices)]
    rise = [(i, (i + 2) % devices) for i in range(devices)]
    fall = [(i, (i - 2) % devices) for i in range(devices)]

    def move(x, pairs):
        return lax.ppermute(x, "blk", pairs)

    def vmem(*lead):
        return pltpu.VMEM((*lead, ROWS, LANES), F32)

    full = (ROWS, LANES)
    pop, scal = interleave(populations), interleave(scalars)
    old, new = interleave(coarse_old), interleave(coarse_new)
    side_table, z_table = reduce_tables()
    own = call(
        begin_kernel,
        "shhhhhhh",
        [shape_of(FIELDS, *full)],
        "v",
        [pltpu.VMEM(x.shape, F32) for x in (pop, scal, old, new)]
        + [pltpu.SMEM(x.shape, x.dtype) for x in (levels, neighbours, relax_rates)]
        + [pltpu.SemaphoreType.DMA((10,))],
        "begin",
        12,
        1 << 27,
    )(info, *[pltpu.with_memory_space_constraint(x, pltpu.HBM) for x in (levels, neighbours, relax_rates, pop, scal, old, new)])[0]
    other = move(own, swap)
    face = pltpu.VMEM((8, 27, CHUNK, LANES), F32)
    held, up, down, near = call(
        plane_kernel,
        "sssvv",
        [shape_of(8, 27, *full), shape_of(9, *full), shape_of(9, *full), jax.ShapeDtypeStruct((8, 6), jnp.int32)],
        "vvvs",
        [vmem(8, 27), face, pltpu.SMEM((8, LANES), F32), pltpu.SemaphoreType.DMA],
        "plane",
        16,
        1 << 27,
    )(info, levels, neighbours, own, other)
    up_in, down_in = move(up, rise), move(down, fall)
    flow, species, up, down, sides = call(
        middle_kernel,
        "ssssssvvvvvv",
        [shape_of(8, 27, *full), shape_of(8, 9, *full), shape_of(8, *full), shape_of(8, *full), shape_of(4, 2304)],
        "vvvvv",
        [
            vmem(8, 27), vmem(8, 27), vmem(8, 9), face, vmem(3), vmem(8, 2), vmem(8, 2), pltpu.SMEM((2, 8), jnp.int32),
        ],
        "middle",
        28,
        1 << 28,
    )(info, levels, near, relax_rates, diffusivity, stoichiometry, own, other, held, up_in, down_in, side_table)
    up_in, down_in = move(up, rise), move(down, fall)
    pop_out, scal_out, returned = call(
        end_kernel,
        "sssssvvvvvvvv",
        [shape_of(27, 128, LANES), shape_of(9, 128, LANES), shape_of(4, 3456)],
        "hhv",
        [pltpu.VMEM(pop.shape, F32), pltpu.VMEM(scal.shape, F32), vmem(4, 3), pltpu.SemaphoreType.DMA((5,))],
        "end",
        20,
        1 << 27,
    )(
        info, levels, neighbours, diffusivity, stoichiometry, flow, species, up_in, down_in, sides, z_table, pop, scal
    )
    return separate(pop_out), separate(scal_out), returned


def solution(mesh):
    in_specs = (
        P("blk", None, None), P("blk", None, None), P("blk", None, None), P("blk", None, None),
        P(), P("blk", None), P(), P(), P(),
    )
    out_specs = (P("blk", None, None), P("blk", None, None), P("blk", None))
    return jax.shard_map(local, mesh=mesh, in_specs=in_specs, out_specs=out_specs, check_vma=False)
```

time: 595 us -> 56 us (0.09); the launches traced: 584 us -> 55.9 us
  local copies, waits for them, and re-layouts: 357 us -> 0.05 us
  other arithmetic: 90.3 us -> 0.08 us
  starting transfers between devices: 101 us -> 18.9 us
  Pallas kernels: 0 us -> 25.9 us
  matrix products: 22.8 us -> 0 us
    another operation x85 -> x0, local copies, waits for them, and re-layouts: 107 us -> none  [the longest x20 62.4 us: spread_face(): tiled = jnp.tile(square_face, (1,) * (len(lead) + 1) + (extent,))]
    slice x87 -> x0, local copies, waits for them, and re-layouts: 96.1 us -> none  [the longest x20 39.2 us: layer_of(): lax.slice_in_dim(flat, index, flat.shape[-1], stride=extent, axis=last_axis)]
    ppermute x44 -> x5, starting transfers between devices: 101 us -> 18.9 us  [move(): return lax.ppermute(x, 'blk', pairs)]
    reshape x22 -> x0, local copies, waits for them, and re-layouts: 46.3 us -> none  [the longest x8 37 us: spread_face(): return jnp.repeat(face, extent, axis=len(lead))]
    gather x51 -> x0, local copies, waits for them, and re-layouts: 39.7 us -> none  [the longest x20 22.2 us: side_values(): nearby[distance[:, facing] + base, positions[:, facing], facing ^ 1]]
    broadcast_in_dim x33 -> x0, local copies, waits for them, and re-layouts: 32.6 us -> none  [the longest x8 27 us: spread_face(): return jnp.repeat(face, extent, axis=len(lead))]
    another operation x41 -> x1, other arithmetic: 32.4 us -> 0.08 us  [local(): info = jnp.stack([me // 2, me % 2]).astype(jnp.int32)]
    pallas_call x0 -> x4, Pallas kernels: none -> 25.9 us  [the longest x1 12.3 us: local(): call(middle_kernel, 'ssssssvvvvvv', [shape_of(8, 27, *full), shape_of(8,...]
  transfers between devices with their start and end apart: 44 -> 5, of which waited for: 7 -> 3; matrix products, arithmetic and copies ran while one was open for 64% -> 0% of each run, Pallas kernels for 0% -> 0%
where the time goes in v1:
time: 56 us; the launch traced here: 55.9 us
  Pallas kernels  25.9 us (46%)
  starting transfers between devices  18.9 us (34%)
  waiting for transfers between devices  10.2 us (18%)
  between operations  0.78 us (1%)
    ppermute x5, starting transfers between devices, move(): return lax.ppermute(x, 'blk', pairs)  18.9 us
    pallas_call x1, Pallas kernels, local(): call(middle_kernel, 'ssssssvvvvvv', [shape_of(8, 27, *full), shape_of(8,...  12.3 us
    ppermute x5, waiting for transfers between devices, move(): return lax.ppermute(x, 'blk', pairs)  10.2 us
    pallas_call x1, Pallas kernels, local(): call(end_kernel, 'sssssvvvvvvvv', [shape_of(27, 128, LANES), shape_of(9,...  5.41 us
    pallas_call x1, Pallas kernels, local(): call(plane_kernel, 'sssvv', [shape_of(8, 27, *full), shape_of(9, *full),...  5.29 us
    pallas_call x1, Pallas kernels, local(): call(begin_kernel, 'shhhhhhh', [shape_of(FIELDS, *full)], 'v', [pltpu.VME...  2.88 us
  transfers between devices with their start and end apart: 5, of which 3 were waited for; matrix products, arithmetic and copies ran while one was open for 0% of the time, Pallas kernels for 0%

profile of v1, /device:TPU:1, one launch (start us, length us, event | category | flops | bytes accessed | tf_op | source)
XLA Modules:
  0.0 55.9 jit_solution(13495937593849217507)
XLA Ops:
  0.6 0.1 pad_add_fusion.info
  0.7 0.0 copy-start.4
  0.7 2.9 %begin.1.own = f32[145,32,128]{2,1,0:T(8,128)S(1)} custom-call(s32[2]{0:T(128)S(1)} %pad_add_fusion.info, s32[1024]{0:T(1024)} %levels.5, s32[4,6]{1,0:T(4,128)} %near.3, f32[27]{0:T(128)} %rates.1, f32[27,128,128]{2,1,0:T(8,128)} %bitcast.32, f32[9,128,128]{2,1,0:T(8,128)} %bitcast.34, f32[27,16,128]{2,1,0:T(8,128)} %bitcast.36, f32[27,16,128]{2,1,0:T(8,128)} %bitcast.37), custom_call_target="tpu_custom_call" | custom-call | flops 134217728 | bytes 8388608 | tf_op jit(solution)/shard_map/begin/pallas_call | solution.py:718
  3.6 0.0 copy-start.2
  3.6 0.0 copy-start.6
  3.6 0.0 copy-start.7
  3.7 0.0 copy-start.8
  3.7 3.2 %collective-permute-start = (f32[145,32,128]{2,1,0:T(8,128)S(1)}, f32[145,32,128]{2,1,0:T(8,128)S(1)}, u32[]{:S(2)}, u32[]{:S(2)}) collective-permute-start(f32[145,32,128]{2,1,0:T(8,128)S(1)} %begin.1.own), channel_id=1, source_target_pairs={{0,1},{1,0},{2,3},{3,2},{4,5},{5,4},{6,7},{7,6},{8,9},{9,8},{10,11... | collective-permute-start | bytes 7127048 | tf_op jit(solution)/shard_map/ppermute | solution.py:709
  6.9 4.2 %collective-permute-done.other = f32[145,32,128]{2,1,0:T(8,128)S(1)} collective-permute-done((f32[145,32,128]{2,1,0:T(8,128)S(1)}, f32[145,32,128]{2,1,0:T(8,128)S(1)}, u32[]{:S(2)}, u32[]{:S(2)}) %collective-permute-start) | collective-permute-done | bytes 2375712 | tf_op jit(solution)/shard_map/ppermute | solution.py:709
  11.1 0.0 copy-done.4
  11.1 0.0 copy-done.5
  11.1 5.3 %plane.1 = (f32[8,27,32,128]{3,2,1,0:T(8,128)S(1)}, f32[9,32,128]{2,1,0:T(8,128)S(1)}, f32[9,32,128]{2,1,0:T(8,128)S(1)}, s32[8,6]{1,0:T(8,128)S(1)}) custom-call(s32[2]{0:T(128)S(1)} %pad_add_fusion.info, s32[1024]{0:T(1024)S(1)} %copy-done.4, s32[4,6]{1,0:T(4,128)S(1)} %copy-done.5, f32[145,32,128]{2,1,0:T(8,128)S(1)} %begin.1.own, ...), custom_call_target="tpu_custom_call" | custom-call | flops 134217728 | bytes 8388608 | tf_op jit(solution)/shard_map/plane/pallas_call | solution.py:732
  16.4 0.1 collective-permute-start.1
  16.5 8.4 %collective-permute-start.2 = (f32[9,32,128]{2,1,0:T(8,128)S(1)}, f32[9,32,128]{2,1,0:T(8,128)S(1)}, u32[]{:S(2)}, u32[]{:S(2)}) collective-permute-start(f32[9,32,128]{2,1,0:T(8,128)S(1)} %get-tuple-element.18), channel_id=1, source_target_pairs={{0,254},{1,255},{2,0},{3,1},{4,2},{5,3},{6,4},{7,5},{8,6},{9,7},{1... | collective-permute-start | bytes 442376 | tf_op jit(solution)/shard_map/ppermute | solution.py:709
  24.8 3.8 %collective-permute-done.1.up_in = f32[9,32,128]{2,1,0:T(8,128)S(1)} collective-permute-done((f32[9,32,128]{2,1,0:T(8,128)S(1)}, f32[9,32,128]{2,1,0:T(8,128)S(1)}, u32[]{:S(2)}, u32[]{:S(2)}) %collective-permute-start.1) | collective-permute-done | bytes 147488 | tf_op jit(solution)/shard_map/ppermute | solution.py:709
  28.6 0.0 collective-permute-done.2.down_in
  28.6 0.0 copy-done.2
  28.6 0.0 copy-done.6
  28.6 0.0 copy-done.7
  28.6 0.0 copy-done.8
  28.6 0.0 copy-start
  28.6 0.0 copy-start.1
  28.6 0.0 copy-start.3
  28.6 12.3 %middle.1 = (f32[8,27,32,128]{3,2,1,0:T(8,128)S(1)}, f32[8,9,32,128]{3,2,1,0:T(8,128)S(1)}, f32[8,32,128]{2,1,0:T(8,128)S(1)}, f32[8,32,128]{2,1,0:T(8,128)S(1)}, f32[4,2304]{1,0:T(4,128)S(1)}) custom-call(s32[2]{0:T(128)S(1)} %pad_add_fusion.info, s32[1024]{0:T(1024)S(1)} %copy-done.4, s32[8,6]{1,0:T(8,128)S(1)} %get-tuple-element.15.near, ...), custom_call_target="tpu_custom_call" | custom-call | flops 268435456 | bytes 8388608 | tf_op jit(solution)/shard_map/middle/pallas_call | solution.py:743
  41.0 0.1 collective-permute-start.3
  41.1 7.2 %collective-permute-start.4 = (f32[8,32,128]{2,1,0:T(8,128)S(1)}, f32[8,32,128]{2,1,0:T(8,128)S(1)}, u32[]{:S(2)}, u32[]{:S(2)}) collective-permute-start(f32[8,32,128]{2,1,0:T(8,128)S(1)} %get-tuple-element.22), channel_id=1, source_target_pairs={{0,254},{1,255},{2,0},{3,1},{4,2},{5,3},{6,4},{7,5},{8,6},{9,7},{1... | collective-permute-start | bytes 393224 | tf_op jit(solution)/shard_map/ppermute | solution.py:709
  48.2 2.3 %collective-permute-done.3.up_in = f32[8,32,128]{2,1,0:T(8,128)S(1)} collective-permute-done((f32[8,32,128]{2,1,0:T(8,128)S(1)}, f32[8,32,128]{2,1,0:T(8,128)S(1)}, u32[]{:S(2)}, u32[]{:S(2)}) %collective-permute-start.3) | collective-permute-done | bytes 131104 | tf_op jit(solution)/shard_map/ppermute | solution.py:709
  50.5 0.0 collective-permute-done.4.down_in
  50.5 0.0 copy-done
  50.5 0.0 copy-done.1
  50.5 0.0 copy-done.3
  50.5 5.4 %end.1 = (f32[27,128,128]{2,1,0:T(8,128)}, f32[9,128,128]{2,1,0:T(8,128)}, f32[4,3456]{1,0:T(4,128)}) custom-call(s32[2]{0:T(128)S(1)} %pad_add_fusion.info, s32[1024]{0:T(1024)S(1)} %copy-done.4, s32[4,6]{1,0:T(4,128)S(1)} %copy-done.5, f32[9]{0:T(128)S(1)} %copy-done.7, f32[9]{0:T(128)S(1)} %copy-done.8, f32[8,27,32,128]{3,2,1,0:T(8,128)S(1)} %get-tuple-element.19.held, ...), custom_call_target="tpu_custom_call" | custom-call | flops 134217728 | bytes 8388608 | tf_op jit(solution)/shard_map/end/pallas_call | solution.py:756
  (1 shorter events, 0.0 us)
Async XLA Ops:
  0.7 10.3 %copy-start.4 = (s32[1024]{0:T(1024)S(1)}, s32[1024]{0:T(1024)}, u32[]{:S(2)}) copy-start(s32[1024]{0:T(1024)} %levels.5) | copy-start | bytes 12292
  0.7 10.3 %copy-start.5 = (s32[4,6]{1,0:T(4,128)S(1)}, s32[4,6]{1,0:T(4,128)}, u32[]{:S(2)}) copy-start(s32[4,6]{1,0:T(4,128)} %near.3) | copy-start | bytes 292
  3.6 25.0 %copy-start.2 = (f32[384,640]{1,0:T(8,128)S(1)}, f32[384,640]{1,0:T(8,128)}, u32[]{:S(2)}) copy-start(f32[384,640]{1,0:T(8,128)} %constant.32.clone.tables) | copy-start | bytes 2949124
  3.6 25.0 %copy-start.6 = (f32[27]{0:T(128)S(1)}, f32[27]{0:T(128)}, u32[]{:S(2)}) copy-start(f32[27]{0:T(128)} %rates.1) | copy-start | bytes 328
  3.6 25.0 %copy-start.7 = (f32[9]{0:T(128)S(1)}, f32[9]{0:T(128)}, u32[]{:S(2)}) copy-start(f32[9]{0:T(128)} %diffusivity.3) | copy-start | bytes 112
  3.7 25.0 %copy-start.8 = (f32[9]{0:T(128)S(1)}, f32[9]{0:T(128)}, u32[]{:S(2)}) copy-start(f32[9]{0:T(128)} %stoichiometry.3) | copy-start | bytes 112
  3.7 7.4 %collective-permute-start = (f32[145,32,128]{2,1,0:T(8,128)S(1)}, f32[145,32,128]{2,1,0:T(8,128)S(1)}, u32[]{:S(2)}, u32[]{:S(2)}) collective-permute-start(f32[145,32,128]{2,1,0:T(8,128)S(1)} %begin.1.own), channel_id=1, source_target_pairs={{0,1},{1,0},{2,3},{3,2},{4,5},{5,4},{6,7},{7,6},{8,9},{9,8},{10,11... | collective-permute-start | bytes 7127048 | tf_op jit(solution)/shard_map/ppermute | solution.py:709
  16.4 12.2 %collective-permute-start.1 = (f32[9,32,128]{2,1,0:T(8,128)S(1)}, f32[9,32,128]{2,1,0:T(8,128)S(1)}, u32[]{:S(2)}, u32[]{:S(2)}) collective-permute-start(f32[9,32,128]{2,1,0:T(8,128)S(1)} %get-tuple-element.17), channel_id=1, source_target_pairs={{0,2},{1,3},{2,4},{3,5},{4,6},{5,7},{6,8},{7,9},{8,10},{9,11},{10,... | collective-permute-start | bytes 442376 | tf_op jit(solution)/shard_map/ppermute | solution.py:709
  16.5 12.1 %collective-permute-start.2 = (f32[9,32,128]{2,1,0:T(8,128)S(1)}, f32[9,32,128]{2,1,0:T(8,128)S(1)}, u32[]{:S(2)}, u32[]{:S(2)}) collective-permute-start(f32[9,32,128]{2,1,0:T(8,128)S(1)} %get-tuple-element.18), channel_id=1, source_target_pairs={{0,254},{1,255},{2,0},{3,1},{4,2},{5,3},{6,4},{7,5},{8,6},{9,7},{1... | collective-permute-start | bytes 442376 | tf_op jit(solution)/shard_map/ppermute | solution.py:709
  28.6 21.9 %copy-start = (f32[4,27,4096]{2,0,1:T(4,128)S(1)}, f32[4,27,4096]{2,0,1:T(4,128)}, u32[]{:S(2)}) copy-start(f32[4,27,4096]{2,0,1:T(4,128)} %param.11) | copy-start | bytes 5308420
  28.6 21.9 %copy-start.1 = (f32[4,9,4096]{2,0,1:T(4,128)S(1)}, f32[4,9,4096]{2,0,1:T(4,128)}, u32[]{:S(2)}) copy-start(f32[4,9,4096]{2,0,1:T(4,128)} %param.12) | copy-start | bytes 1769476
  28.6 21.9 %copy-start.3 = (f32[128,640]{1,0:T(8,128)S(1)}, f32[128,640]{1,0:T(8,128)}, u32[]{:S(2)}) copy-start(f32[128,640]{1,0:T(8,128)} %constant.33.clone.table) | copy-start | bytes 983044
  41.0 9.5 %collective-permute-start.3 = (f32[8,32,128]{2,1,0:T(8,128)S(1)}, f32[8,32,128]{2,1,0:T(8,128)S(1)}, u32[]{:S(2)}, u32[]{:S(2)}) collective-permute-start(f32[8,32,128]{2,1,0:T(8,128)S(1)} %get-tuple-element.21), channel_id=1, source_target_pairs={{0,2},{1,3},{2,4},{3,5},{4,6},{5,7},{6,8},{7,9},{8,10},{9,11},{10,... | collective-permute-start | bytes 393224 | tf_op jit(solution)/shard_map/ppermute | solution.py:709
  41.1 9.4 %collective-permute-start.4 = (f32[8,32,128]{2,1,0:T(8,128)S(1)}, f32[8,32,128]{2,1,0:T(8,128)S(1)}, u32[]{:S(2)}, u32[]{:S(2)}) collective-permute-start(f32[8,32,128]{2,1,0:T(8,128)S(1)} %get-tuple-element.22), channel_id=1, source_target_pairs={{0,254},{1,255},{2,0},{3,1},{4,2},{5,3},{6,4},{7,5},{8,6},{9,7},{1... | collective-permute-start | bytes 393224 | tf_op jit(solution)/shard_map/ppermute | solution.py:709

commit v2 on v1

--- a/solution.py
+++ b/solution.py
@@ -116,7 +116,7 @@
 
 
 def begin_kernel(
-    info, levels_in, near_in, rates_in, pop, scal, old, new, out,
+    info, levels_in, near_in, rates_in, pop, scal, old, new, out, up, down,
     pops, scals, olds, news, levels, near, rates, sems,
 ):
     layer, core = info[0], info[1]
@@ -142,7 +142,7 @@
     meta = jnp.zeros((CHUNK, LANES), F32)
     for b in range(4):
         for q in range(6):
-            here = jnp.logical_and(row == b, lane == q)
+            here = jnp.logical_and(row == b, lane == q + 8)
             meta = jnp.where(here, near[b, q].astype(F32), meta)
     out[FIELDS - 1, 0:8, :] = meta
 
@@ -183,6 +183,24 @@
                     out[b * PER_BLOCK + p, pl.ds(8 * v, 8), :] = grow_row(before, index)
 
 
+    pack_faces(out, up, down, meta)
+
+
+def pack_faces(out, up, down, meta=None):
+    lane = iota(CHUNK, 1) % 16
+
+    @pl.loop(0, 4)
+    def _(v):
+        at = chunk_at(v)
+        for ref, digit, start in ((up, 2, 15), (down, 0, 0)):
+            for b in range(4):
+                fields = [out[b * PER_BLOCK + 3 * e + digit, at, :] for e in range(9)]
+                fields += [out[b * PER_BLOCK + 27 + e, at, :] for e in range(7)]
+                ref[b, at, :] = pack_into(fields, 0, start, lane)
+            rest = pack_into([out[b * PER_BLOCK + 34 + e, at, :] for b in range(4) for e in range(2)], 0, start, lane)
+            ref[4, at, :] = rest if meta is None else jnp.where(lane < 8, rest, meta)
+
+
 def spot(block, core):
     return (block % 8) ^ (core * 4)
 
@@ -218,52 +236,49 @@
         ref[(*lead, pl.ds(8 * v, 8), slice(None))] = values[v]
 
 
-def sections_xy(halves, faces, mid, dest, near, core, fine_of):
+def sections_xy(refs, faces, mid, dest, near, core, fine_of):
     row = iota(CHUNK, 0)
     even = row % 2 == 0
     group = iota(CHUNK, 1) // 16
 
-    for half, field in enumerate(halves):
+    for half, ref in enumerate(refs):
 
         @pl.loop(0, 4)
         def _(i):
             for p, c in enumerate(VEL):
-                ref, lead = field(i, p)
                 if c[0] == 1:
-                    faces[half * 4 + i, p] = pltpu.roll(ref[(*lead, pl.ds(24, 8), slice(None))], 2, 0)
+                    faces[half * 4 + i, p] = pltpu.roll(ref[i * PER_BLOCK + p, pl.ds(24, 8), :], 2, 0)
                 elif c[0] == -1:
-                    faces[half * 4 + i, p] = pltpu.roll(ref[(*lead, pl.ds(0, 8), slice(None))], CHUNK - 2, 0)
-
-    for half, field in enumerate(halves):
+                    faces[half * 4 + i, p] = pltpu.roll(ref[i * PER_BLOCK + p, pl.ds(0, 8), :], CHUNK - 2, 0)
+
+    for half, ref in enumerate(refs):
 
         @pl.loop(0, 4)
         def _(i):
             b = half * 4 + i
             fine = fine_of(b)
+            fields = [p for p in range(27) if half == 0 or VEL[p][1] != 0]
 
             @pl.when(fine)
             def _():
                 low, high = spot(near[b, 0], core), spot(near[b, 1], core)
-                for p, c in enumerate(VEL):
-                    ref, lead = field(i, p)
-                    values = chunks(ref, *lead)
-                    if c[0] == 1:
+                for p in fields:
+                    values = chunks(ref, i * PER_BLOCK + p)
+                    if VEL[p][0] == 1:
                         values = x_up(values, faces[low, p], row)
-                    elif c[0] == -1:
+                    elif VEL[p][0] == -1:
                         values = x_down(values, faces[high, p], row)
                     put(mid, (b, p), values)
 
             @pl.when(jnp.logical_not(fine))
             def _():
-                for p in range(27):
-                    ref, lead = field(i, p)
-                    put(mid, (b, p), chunks(ref, *lead))
-
-    @pl.loop(0, 8)
+                for p in fields:
+                    if VEL[p][1] != 0:
+                        put(mid, (b, p), chunks(ref, i * PER_BLOCK + p))
+
+    @pl.loop(0, 4)
     def _(b):
-        fine = fine_of(b)
-
-        @pl.when(fine)
+        @pl.when(fine_of(b))
         def _():
             low, high = spot(near[b, 2], core), spot(near[b, 3], core)
             for p, c in enumerate(VEL):
@@ -276,12 +291,6 @@
                         value = y_down(value, mid[high, p, at, :], even, group)
                     dest[b, p, at, :] = value
 
-        @pl.when(jnp.logical_not(fine))
-        def _():
-            for p in range(27):
-                if VEL[p][2] != 0:
-                    put(dest, (b, p), chunks(mid, b, p))
-
 
 def pack_into(fields, first_slot, start, lane):
     out = None
@@ -292,11 +301,7 @@
     return out
 
 
-def halves_of(own, other):
-    return [lambda i, p: (own, (i * PER_BLOCK + p,)), lambda i, p: (other, (i * PER_BLOCK + p,))]
-
-
-def plane_kernel(info, levels, near, own, other, dest, up, down, table, mid, faces, meta, sem):
+def plane_kernel(info, levels, near, own, other, dest, table, mid, faces, meta, sem):
     layer, core = info[0], info[1]
     copy = pltpu.make_async_copy(other.at[FIELDS - 1, pl.ds(0, 8), :], meta, sem)
     copy.start()
@@ -304,31 +309,77 @@
     for i in range(4):
         for q in range(6):
             table[i, q] = near[i, q]
-            table[4 + i, q] = meta[i, q].astype(jnp.int32)
+            table[4 + i, q] = meta[i, 8 + q].astype(jnp.int32)
 
     def fine_of(b):
         return levels[layer * 8 + spot(b, core)] == 1
 
-    sections_xy(halves_of(own, other), faces, mid, dest, table, core, fine_of)
-    lane = iota(CHUNK, 1) % 16
-
-    for half, ref_in in enumerate((own, other)):
-
-        @pl.loop(0, 4)
-        def _(i):
-            b = half * 4 + i
-            for v in range(4):
-                at = pl.ds(8 * v, 8)
-                for ref, digit, start in ((up, 2, 15), (down, 0, 0)):
-                    fields = [dest[b, 3 * e + digit, at, :] for e in range(9)]
-                    fields += [ref_in[i * PER_BLOCK + 27 + e, at, :] for e in range(7)]
-                    ref[b, at, :] = pack_into(fields, 0, start, lane)
-                    held = ref[8, at, :]
-                    for e in range(2):
-                        slot = 2 * b + e
-                        moved = pltpu.roll(ref_in[i * PER_BLOCK + 34 + e, at, :], (slot - start) % LANES, 1)
-                        held = jnp.where(lane == slot, moved, held)
-                    ref[8, at, :] = held
+    sections_xy((own, other), faces, mid, dest, table, core, fine_of)
+
+
+def arrive(info, levels, table, core, incoming, raw, mid, done):
+    row, slot = iota(CHUNK, 0), iota(CHUNK, 1) % 16
+    even, group = row % 2 == 0, iota(CHUNK, 1) // 16
+    x_plus, x_minus = jnp.logical_and(slot >= 6, slot < 9), slot < 3
+    y_plus = jnp.logical_and(slot < 9, slot % 3 == 2)
+    y_minus = jnp.logical_and(slot < 9, slot % 3 == 0)
+    for way in range(2):
+        for half in range(2):
+            for i in range(4):
+                put(raw, (way, half * 4 + i), chunks(incoming[way][half], i))
+
+    for way in range(2):
+
+        @pl.loop(0, 8)
+        def _(b):
+            fine = levels[info[2 + way] * 8 + spot(b, core)] == 1
+            own = chunks(raw, way, b)
+
+            @pl.when(fine)
+            def _():
+                low, high = spot(table[way * 8 + b, 0], core), spot(table[way * 8 + b, 1], core)
+                before = x_up(own, pltpu.roll(raw[way, low, pl.ds(24, 8), :], 2, 0), row)
+                after = x_down(own, pltpu.roll(raw[way, high, pl.ds(0, 8), :], CHUNK - 2, 0), row)
+                values = [jnp.where(x_plus, x, jnp.where(x_minus, y, z)) for x, y, z in zip(before, after, own)]
+                put(mid, (way, b), values)
+
+            @pl.when(jnp.logical_not(fine))
+            def _():
+                put(mid, (way, b), own)
+
+    for way in range(2):
+
+        @pl.loop(0, 8)
+        def _(b):
+            fine = levels[info[2 + way] * 8 + spot(b, core)] == 1
+            own = chunks(mid, way, b)
+
+            @pl.when(fine)
+            def _():
+                low, high = spot(table[way * 8 + b, 2], core), spot(table[way * 8 + b, 3], core)
+                values = []
+                for v, here in enumerate(own):
+                    at = pl.ds(8 * v, 8)
+                    before = y_up(here, mid[way, low, at, :], even, group)
+                    after = y_down(here, mid[way, high, at, :], even, group)
+                    values.append(jnp.where(y_plus, before, jnp.where(y_minus, after, here)))
+                put(done, (way, b), values)
+
+            @pl.when(jnp.logical_not(fine))
+            def _():
+                put(done, (way, b), own)
+
+
+def face_reader(done, rest, below, above):
+    def faces(m, at):
+        if m < 7:
+            slot = 9 + m
+            return roll_lanes(done[0, below, at, :], -slot), roll_lanes(done[1, above, at, :], 15 - slot)
+        low = LANES - 2 * (below % 4) - (m - 7)
+        high = (LANES + 15 - 2 * (above % 4) - (m - 7)) % LANES
+        return pltpu.roll(rest[0, below // 4, at, :], low, 1), pltpu.roll(rest[1, above // 4, at, :], high, 1)
+
+    return faces
 
 
 def z_section(h, up, down, depth):
@@ -424,21 +475,25 @@
 
 
 def middle_kernel(
-    info, levels, near, rates, diffusivity, stoichiometry, own, other, held, up_in, down_in, tables,
-    flow, species, up, down, sides_out,
-    first, mid, old, faces, flux, edge_x, edge_y, inverse,
+    info, levels, near, rates, diffusivity, stoichiometry, own, other, held, up_own, up_other, down_own, down_other,
+    out, up, down, table,
+    raw, mid, done, rest, old, flux, metas, sems,
 ):
     layer, core = info[0], info[1]
     index = grow_index()
-    depth = iota(CHUNK, 1) % 16
+    incoming = ((up_own, up_other), (down_own, down_other))
+    copies = []
+    for way in range(2):
+        for half in range(2):
+            k = way * 2 + half
+            copies.append(
+                pltpu.make_async_copy(incoming[way][half].at[4, pl.ds(0, 8), :], metas.at[k], sems.at[k])
+            )
+            copies[-1].start()
+            put(rest, (way, half), chunks(incoming[way][half], 4))
 
     def fine_of(b):
         return levels[layer * 8 + spot(b, core)] == 1
-
-    @pl.loop(0, 8)
-    def _(b):
-        inverse[0, spot(near[b, 5], core)] = b
-        inverse[1, spot(near[b, 4], core)] = b
 
     for half, ref_in in enumerate((own, other)):
 
@@ -447,14 +502,15 @@
             for m in range(9):
                 put(old, (half * 4 + i, m), chunks(ref_in, i * PER_BLOCK + 27 + m))
 
-            @pl.when(jnp.logical_not(fine_of(half * 4 + i)))
-            def _():
-                for p in range(27):
-                    for v in range(4):
-                        line = ref_in[i * PER_BLOCK + 27 + p // 8, pl.ds(p % 8 * 4 + v, 1), :]
-                        first[half * 4 + i, p, pl.ds(8 * v, 8), :] = grow_row(line, index)
-
-    @pl.loop(0, 8)
+    for copy in copies:
+        copy.wait()
+    for way in range(2):
+        for b in range(8):
+            for q in range(6):
+                table[way * 8 + b, q] = metas[way * 2 + b // 4, b % 4, 8 + q].astype(jnp.int32)
+    arrive(info, levels, table, core, incoming, raw, mid, done)
+
+    @pl.loop(0, 4)
     def _(b):
         @pl.when(fine_of(b))
         def _():
@@ -463,82 +519,93 @@
             @pl.loop(0, 4)
             def _(v):
                 at = chunk_at(v)
-                g = z_section(lambda p: held[b, p, at, :], up_in[below, at, :], down_in[above, at, :], depth)
+                g = z_section(lambda p: held[b, p, at, :], done[0, below, at, :], done[1, above, at, :], depth_of())
                 post, j = collide(g, lambda k: rates[k])
                 for p in range(27):
-                    first[b, p, at, :] = post[p]
+                    out[b * PER_BLOCK + p, at, :] = post[p]
                 for d in range(3):
                     flux[d, at, :] = j[d] * (0.5 / 216.0)
 
-            def z_faces(m, at):
-                if m < 7:
-                    slot = 9 + m
-                    return roll_lanes(up_in[below, at, :], -slot), roll_lanes(down_in[above, at, :], 15 - slot)
-                low = LANES - 2 * below - (m - 7)
-                high = (LANES + 15 - 2 * above - (m - 7)) % LANES
-                return pltpu.roll(up_in[8, at, :], low, 1), pltpu.roll(down_in[8, at, :], high, 1)
-
             def store(m, v, value):
-                species[b, m, pl.ds(8 * v, 8), :] = value
+                out[b * PER_BLOCK + 27 + m, pl.ds(8 * v, 8), :] = value
 
             species_step(
-                old, b, [spot(near[b, q], core) for q in range(4)], z_faces, flux,
+                old, b, [spot(near[b, q], core) for q in range(4)], face_reader(done, rest, below, above), flux,
                 [levels[near[b, q]] for q in range(6)], diffusivity, stoichiometry, store,
             )
 
         @pl.when(jnp.logical_not(fine_of(b)))
         def _():
-            species[b] = jnp.zeros((9, ROWS, LANES), F32)
-
-    sections_xy([lambda i, p: (first, (i, p)), lambda i, p: (first, (4 + i, p))], faces, mid, flow, near, core, fine_of)
-
-    for way, (ref, digit, start) in enumerate(((up, 2, 15), (down, 0, 0))):
-        for half, ref_in in enumerate((own, other)):
-
-            @pl.loop(0, 4)
-            def _(i):
-                b = half * 4 + i
-                target = spot(near[b, 5 - way], core)
-
-                @pl.when(target < 4)
-                def _():
-                    for v in range(4):
-                        at = pl.ds(8 * v, 8)
-                        fields = [flow[b, 3 * e + digit, at, :] for e in range(9)]
-                        fields += [species[b, e, at, :] for e in range(7)]
-                        ref[2 * target, at, :] = pack_into(fields, 0, start, depth)
-                        fields = [
-                            0.125 * (ref_in[i * PER_BLOCK + 3 * e + digit, at, :] + first[b, 3 * e + digit, at, :])
-                            for e in range(9)
-                        ]
-                        fields += [species[b, 7, at, :], species[b, 8, at, :]]
-                        ref[2 * target + 1, at, :] = pack_into(fields, 0, start, depth)
-
+            for p in range(27):
+                for v in range(4):
+                    line = own[b * PER_BLOCK + 27 + p // 8, pl.ds(p % 8 * 4 + v, 1), :]
+                    out[b * PER_BLOCK + p, pl.ds(8 * v, 8), :] = grow_row(line, index)
+            for m in range(9):
+                put(out, (b * PER_BLOCK + 27 + m,), [jnp.zeros((CHUNK, LANES), F32)] * 4)
+
+    pack_faces(out, up, down)
+    row, lane = iota(CHUNK, 0), iota(CHUNK, 1)
+
+    @pl.loop(0, 4)
+    def _(v):
+        at = chunk_at(v)
+        for ref, digit, start in ((up, 2, 15), (down, 0, 0)):
+            merged = None
+            for b in range(4):
+                fields = [
+                    0.125 * (own[b * PER_BLOCK + 3 * e + digit, at, :] + out[b * PER_BLOCK + 3 * e + digit, at, :])
+                    for e in range(9)
+                ]
+                total = pack_into(fields, 0, start, lane % 16)
+                total = total + pltpu.roll(total, CHUNK - 2, 0)
+                total = total + roll_lanes(total, -16)
+                if b % 2:
+                    total = pltpu.roll(total, 2, 0)
+                if b // 2:
+                    total = roll_lanes(total, 16)
+                here = jnp.logical_and(row // 2 % 2 == b % 2, lane // 16 % 2 == b // 2)
+                merged = total if merged is None else jnp.where(here, total, merged)
+            ref[5, at, :] = merged
+
+
+def depth_of():
+    return iota(CHUNK, 1) % 16
+
+
+def second_plane_kernel(
+    info, levels, near, own, other, own_before, other_before, tables, dest, sides_out, mid, faces, edge_x, edge_y
+):
+    layer, core = info[0], info[1]
+
+    def fine_of(b):
+        return levels[layer * 8 + spot(b, core)] == 1
+
+    sections_xy((own, other), faces, mid, dest, near, core, fine_of)
     group, odd = iota(CHUNK, 1) // 16, iota(CHUNK, 0) % 2 == 1
-    for half, ref_in in enumerate((own, other)):
+    for half, (one, two) in enumerate(((own_before, own), (other_before, other))):
 
         @pl.loop(0, 4)
         def _(i):
             b = half * 4 + i
 
+            def total(p, at):
+                return one[i * PER_BLOCK + p, at, :] + two[i * PER_BLOCK + p, at, :]
+
             @pl.when(fine_of(b))
             def _():
                 for side in range(2):
                     at = pl.ds(30, 2) if side == 0 else pl.ds(0, 2)
                     for e in range(9):
-                        p = 18 + e if side == 0 else e
-                        edge_x[b, side, pl.ds(2 * e, 2), :] = ref_in[i * PER_BLOCK + p, at, :] + first[b, p, at, :]
+                        edge_x[b, side, pl.ds(2 * e, 2), :] = total(18 + e if side == 0 else e, at)
                     edge_x[b, side, pl.ds(18, 14), :] = jnp.zeros((14, LANES), F32)
                 for v in range(4):
                     at = pl.ds(8 * v, 8)
                     packs = [None, None]
                     for e in range(9):
                         p_low = 9 * (e // 3) + e % 3
-                        p_high = p_low + 6
-                        high = ref_in[i * PER_BLOCK + p_high, at, :] + first[b, p_high, at, :]
-                        low = ref_in[i * PER_BLOCK + p_low, at, :] + first[b, p_low, at, :]
                         slot = e % 8
-                        both = jnp.where(odd, roll_lanes(high, 16 * (slot - 7)), roll_lanes(low, 16 * slot))
+                        high = roll_lanes(total(p_low + 6, at), 16 * (slot - 7))
+                        both = jnp.where(odd, high, roll_lanes(total(p_low, at), 16 * slot))
                         held_pack = packs[e // 8]
                         packs[e // 8] = both if held_pack is None else jnp.where(group == slot, both, held_pack)
                     for a in range(2):
@@ -549,27 +616,24 @@
     keep_x = jnp.logical_and(row // 2 == e_of, row % 2 == cell // 32)
     keep_y = row // 4 == cell // 8
     odd_row = row % 2 == 1
-
     for s in range(4):
         coarse = jnp.logical_not(fine_of(s))
 
         @pl.when(coarse)
         def _(s=s):
-            weight = [jnp.where(levels[near[s, q]] == 1, 0.125, 0.0) for q in range(4)]
+            fine = [levels[near[s, q]] == 1 for q in range(4)]
             at = [spot(near[s, q], core) for q in range(4)]
             rows = []
             for q in range(2):
-                face = jnp.where(levels[near[s, q]] == 1, edge_x[at[q], q], 0.0)
-                spread = times(face, tables[0:128, :])
-                rows.append(weight[q] * jnp.sum(jnp.where(keep_x, spread, 0.0), axis=0, keepdims=True))
+                spread = times(jnp.where(fine[q], 0.125 * edge_x[at[q], q], 0.0), tables[0:128, :])
+                rows.append(jnp.sum(jnp.where(keep_x, spread, 0.0), axis=0, keepdims=True))
             put_pair(sides_out, s, 0, rows[0], rows[1])
             rows = []
             for q in (2, 3):
-                fine = levels[near[s, q]] == 1
-                spread = times(jnp.where(fine, edge_y[at[q], 0], 0.0), tables[128:256, :])
-                spread += times(jnp.where(fine, edge_y[at[q], 1], 0.0), tables[256:384, :])
+                spread = times(jnp.where(fine[q], 0.125 * edge_y[at[q], 0], 0.0), tables[128:256, :])
+                spread += times(jnp.where(fine[q], 0.125 * edge_y[at[q], 1], 0.0), tables[256:384, :])
                 keep = jnp.logical_and(keep_y, odd_row if q == 2 else jnp.logical_not(odd_row))
-                rows.append(weight[q] * jnp.sum(jnp.where(keep, spread, 0.0), axis=0, keepdims=True))
+                rows.append(jnp.sum(jnp.where(keep, spread, 0.0), axis=0, keepdims=True))
             put_pair(sides_out, s, 1152, rows[0], rows[1])
 
         @pl.when(jnp.logical_not(coarse))
@@ -578,14 +642,29 @@
 
 
 def end_kernel(
-    info, levels, near, diffusivity, stoichiometry, held, species, up_in, down_in, sides, table, pop, scal,
+    info, levels, near, table, diffusivity, stoichiometry, held, own, other,
+    up_own, up_other, down_own, down_other, sides, weights, pop, scal,
     pop_out, scal_out, returned,
-    pops, scals, flux, sems,
+    raw, mid, done, rest, returning, species, pops, scals, flux, sems,
 ):
     layer, core = info[0], info[1]
+    incoming = ((up_own, up_other), (down_own, down_other))
+    for half, ref_in in enumerate((own, other)):
+
+        @pl.loop(0, 4)
+        def _(i):
+            for m in range(9):
+                put(species, (half * 4 + i, m), chunks(ref_in, i * PER_BLOCK + 27 + m))
+
+        for way in range(2):
+            put(rest, (way, half), chunks(incoming[way][half], 4))
+            put(returning, (way, half), chunks(incoming[way][half], 5))
+
+    arrive(info, levels, table, core, incoming, raw, mid, done)
     depth = iota(CHUNK, 1) % 16
     row, col = wide_iota(0), wide_iota(1)
     keep = row // 4 * 2 + row % 2 == col % 64 // 4
+    slim, wide = iota(ROWS, 0), iota(ROWS, 1)
 
     def fine_of(s):
         return levels[layer * 8 + core * 4 + s] == 1
@@ -600,7 +679,8 @@
 
             @pl.when(fine_of(s))
             def _():
-                g = z_section(lambda p: held[s, p, at, :], up_in[2 * s, at, :], down_in[2 * s, at, :], depth)
+                below, above = spot(near[s, 4], core), spot(near[s, 5], core)
+                g = z_section(lambda p: held[s, p, at, :], done[0, below, at, :], done[1, above, at, :], depth)
                 for p in range(27):
                     pops[p, rows, :] = g[p]
                 m = forward_moments(g)
@@ -620,15 +700,12 @@
     def _(s):
         @pl.when(fine_of(s))
         def _():
-            def z_faces(m, at):
-                a, slot = (2 * s, 9 + m) if m < 7 else (2 * s + 1, 2 + m)
-                return roll_lanes(up_in[a, at, :], -slot), roll_lanes(down_in[a, at, :], 15 - slot)
-
             def store(m, v, value):
                 scals[m, pl.ds(32 * v + s, 8, stride=4), :] = value
 
             species_step(
-                species, s, [spot(near[s, q], core) for q in range(4)], z_faces, flux.at[s],
+                species, s, [spot(near[s, q], core) for q in range(4)],
+                face_reader(done, rest, spot(near[s, 4], core), spot(near[s, 5], core)), flux.at[s],
                 [levels[near[s, q]] for q in range(6)], diffusivity, stoichiometry, store,
             )
 
@@ -648,9 +725,12 @@
         @pl.when(coarse)
         def _(s=s):
             rows = []
-            for a, ref in enumerate((up_in, down_in)):
-                face = jnp.where(levels[near[s, 4 + a]] == 1, ref[2 * s + 1], 0.0)
-                rows.append(jnp.sum(jnp.where(keep, times(face, table[...]), 0.0), axis=0, keepdims=True))
+            for way in range(2):
+                m = spot(near[s, 4 + way], core)
+                here = jnp.logical_and(slim // 2 % 2 == m % 2, wide // 16 % 2 == m % 4 // 2)
+                here = jnp.logical_and(here, levels[near[s, 4 + way]] == 1)
+                face = jnp.where(here, returning[way, m // 4], 0.0)
+                rows.append(jnp.sum(jnp.where(keep, times(face, weights[...]), 0.0), axis=0, keepdims=True))
             put_pair(returned, s, 2304, rows[0], rows[1])
 
         @pl.when(jnp.logical_not(coarse))
@@ -700,7 +780,8 @@
 ):
     devices = lax.axis_size("blk")
     me = lax.axis_index("blk")
-    info = jnp.stack([me // 2, me % 2]).astype(jnp.int32)
+    layer, layers = me // 2, devices // 2
+    info = jnp.stack([layer, me % 2, (layer + layers - 1) % layers, (layer + 1) % layers]).astype(jnp.int32)
     swap = [(i, i ^ 1) for i in range(devices)]
     rise = [(i, (i + 2) % devices) for i in range(devices)]
     fall = [(i, (i - 2) % devices) for i in range(devices)]
@@ -715,55 +796,74 @@
     pop, scal = interleave(populations), interleave(scalars)
     old, new = interleave(coarse_old), interleave(coarse_new)
     side_table, z_table = reduce_tables()
-    own = call(
+    fields = FIELDS - 1
+    semaphores = pltpu.SemaphoreType.DMA
+    own, up, down = call(
         begin_kernel,
         "shhhhhhh",
-        [shape_of(FIELDS, *full)],
-        "v",
+        [shape_of(FIELDS, *full), shape_of(5, *full), shape_of(5, *full)],
+        "vvv",
         [pltpu.VMEM(x.shape, F32) for x in (pop, scal, old, new)]
         + [pltpu.SMEM(x.shape, x.dtype) for x in (levels, neighbours, relax_rates)]
-        + [pltpu.SemaphoreType.DMA((10,))],
+        + [semaphores((10,))],
         "begin",
         12,
         1 << 27,
-    )(info, *[pltpu.with_memory_space_constraint(x, pltpu.HBM) for x in (levels, neighbours, relax_rates, pop, scal, old, new)])[0]
+    )(info, *[pltpu.with_memory_space_constraint(x, pltpu.HBM) for x in (levels, neighbours, relax_rates, pop, scal, old, new)])
     other = move(own, swap)
+    up, down = move(up, rise), move(down, fall)
     face = pltpu.VMEM((8, 27, CHUNK, LANES), F32)
-    held, up, down, near = call(
+    held, near = call(
         plane_kernel,
         "sssvv",
-        [shape_of(8, 27, *full), shape_of(9, *full), shape_of(9, *full), jax.ShapeDtypeStruct((8, 6), jnp.int32)],
+        [shape_of(4, 27, *full), jax.ShapeDtypeStruct((8, 6), jnp.int32)],
+        "vs",
+        [vmem(8, 27), face, pltpu.SMEM((8, LANES), F32), semaphores],
+        "plane",
+        12,
+        1 << 27,
+    )(info, levels, neighbours, own, other)
+    held, up, down = lax.optimization_barrier((held, up, down))
+    landing = [vmem(2, 8), vmem(2, 8), vmem(2, 8), vmem(2, 2)]
+    own_next, up_next, down_next, table = call(
+        middle_kernel,
+        "ssssssvvvvvvv",
+        [shape_of(fields, *full), shape_of(6, *full), shape_of(6, *full), jax.ShapeDtypeStruct((16, 6), jnp.int32)],
         "vvvs",
-        [vmem(8, 27), face, pltpu.SMEM((8, LANES), F32), pltpu.SemaphoreType.DMA],
-        "plane",
+        landing + [vmem(8, 9), vmem(3), pltpu.SMEM((4, 8, LANES), F32), semaphores((4,))],
+        "middle",
+        14,
+        1 << 28,
+    )(
+        info, levels, near, relax_rates, diffusivity, stoichiometry, own, other, held,
+        up, move(up, swap), down, move(down, swap),
+    )
+    other_next = move(own_next, swap)
+    up, down = move(up_next, rise), move(down_next, fall)
+    held, sides = call(
+        second_plane_kernel,
+        "sssvvvvv",
+        [shape_of(4, 27, *full), shape_of(4, 2304)],
+        "vv",
+        [vmem(8, 27), face, vmem(8, 2), vmem(8, 2)],
+        "plane2",
+        14,
+        1 << 27,
+    )(info, levels, near, own_next, other_next, own, other, side_table)
+    held, sides, up, down = lax.optimization_barrier((held, sides, up, down))
+    pop_out, scal_out, returned = call(
+        end_kernel,
+        "ssssssvvvvvvvvvvv",
+        [shape_of(27, 128, LANES), shape_of(9, 128, LANES), shape_of(4, 3456)],
+        "hhv",
+        landing
+        + [vmem(2, 2), vmem(8, 9), pltpu.VMEM(pop.shape, F32), pltpu.VMEM(scal.shape, F32), vmem(4, 3), semaphores((5,))],
+        "end",
         16,
         1 << 27,
-    )(info, levels, neighbours, own, other)
-    up_in, down_in = move(up, rise), move(down, fall)
-    flow, species, up, down, sides = call(
-        middle_kernel,
-        "ssssssvvvvvv",
-        [shape_of(8, 27, *full), shape_of(8, 9, *full), shape_of(8, *full), shape_of(8, *full), shape_of(4, 2304)],
-        "vvvvv",
-        [
-            vmem(8, 27), vmem(8, 27), vmem(8, 9), face, vmem(3), vmem(8, 2), vmem(8, 2), pltpu.SMEM((2, 8), jnp.int32),
-        ],
-        "middle",
-        28,
-        1 << 28,
-    )(info, levels, near, relax_rates, diffusivity, stoichiometry, own, other, held, up_in, down_in, side_table)
-    up_in, down_in = move(up, rise), move(down, fall)
-    pop_out, scal_out, returned = call(
-        end_kernel,
-        "sssssvvvvvvvv",
-        [shape_of(27, 128, LANES), shape_of(9, 128, LANES), shape_of(4, 3456)],
-        "hhv",
-        [pltpu.VMEM(pop.shape, F32), pltpu.VMEM(scal.shape, F32), vmem(4, 3), pltpu.SemaphoreType.DMA((5,))],
-        "end",
-        20,
-        1 << 27,
     )(
-        info, levels, neighbours, diffusivity, stoichiometry, flow, species, up_in, down_in, sides, z_table, pop, scal
+        info, levels, neighbours, table, diffusivity, stoichiometry, held, own_next, other_next,
+        up, move(up, swap), down, move(down, swap), sides, z_table, pop, scal,
     )
     return separate(pop_out), separate(scal_out), returned
 

time: 56 us -> 49.9 us (0.89)
  waiting for transfers between devices: 10.2 us -> 2.25 us
  starting transfers between devices: 18.9 us -> 21.7 us
  Pallas kernels: 25.9 us -> 25.1 us
    ppermute x5 -> x10, waiting for transfers between devices: 10.2 us -> 2.25 us  [move(): return lax.ppermute(x, 'blk', pairs)]
    ppermute x5 -> x10, starting transfers between devices: 18.9 us -> 21.7 us  [move(): return lax.ppermute(x, 'blk', pairs)]
    pallas_call x4 -> x5, Pallas kernels: 25.9 us -> 25.1 us  [the longest x1 8.37 us: local(): call(middle_kernel, 'ssssssvvvvvvv', [shape_of(fields, *full), shape_of(6...]
  transfers between devices with their start and end apart: 5 -> 10, of which waited for: 3 -> 4; matrix products, arithmetic and copies ran while one was open for 0% -> 0% of each run, Pallas kernels for 0% -> 13%
where the time goes in v2:
time: 49.9 us; the launch traced here: 50.2 us
  Pallas kernels  25.1 us (50%)
  starting transfers between devices  21.7 us (43%)
  waiting for transfers between devices  2.25 us (5%)
  between operations  0.99 us (2%)
    ppermute x10, starting transfers between devices, move(): return lax.ppermute(x, 'blk', pairs)  21.7 us
    pallas_call x1, Pallas kernels, local(): call(middle_kernel, 'ssssssvvvvvvv', [shape_of(fields, *full), shape_of(6...  8.37 us
    pallas_call x1, Pallas kernels, local(): call(end_kernel, 'ssssssvvvvvvvvvvv', [shape_of(27, 128, LANES), shape_of...  6.43 us
    pallas_call x1, Pallas kernels, local(): call(second_plane_kernel, 'sssvvvvv', [shape_of(4, 27, *full), shape_of(4...  3.76 us
    pallas_call x1, Pallas kernels, local(): call(begin_kernel, 'shhhhhhh', [shape_of(FIELDS, *full), shape_of(5, *ful...  3.67 us
    pallas_call x1, Pallas kernels, local(): call(plane_kernel, 'sssvv', [shape_of(4, 27, *full), jax.ShapeDtypeStruct...  2.91 us
    ppermute x10, waiting for transfers between devices, move(): return lax.ppermute(x, 'blk', pairs)  2.25 us
  transfers between devices with their start and end apart: 10, of which 4 were waited for; matrix products, arithmetic and copies ran while one was open for 0% of the time, Pallas kernels for 13%

profile of v2, /device:TPU:1, one launch (start us, length us, event | category | flops | bytes accessed | tf_op | source)
XLA Modules:
  0.0 50.2 jit_solution(11349552043455195721)
XLA Ops:
  0.6 0.0 copy-start.4
  0.6 0.0 copy-start.5
  0.7 0.1 pad_add_fusion.info
  0.8 3.7 %begin.1 = (f32[145,32,128]{2,1,0:T(8,128)S(1)}, f32[5,32,128]{2,1,0:T(8,128)S(1)}, f32[5,32,128]{2,1,0:T(8,128)S(1)}) custom-call(s32[4]{0:T(128)S(1)} %pad_add_fusion.info, s32[1024]{0:T(1024)} %levels.7, s32[4,6]{1,0:T(4,128)} %near.3, f32[27]{0:T(128)} %rates.1, f32[27,128,128]{2,1,0:T(8,128)} %bitcast.34, f32[9,128,128]{2,1,0:T(8,128)} %bitcast.36, ...), custom_call_target="tpu_custom_call" | custom-call | flops 134217728 | bytes 8388608 | tf_op jit(solution)/shard_map/begin/pallas_call | solution.py:801
  4.5 3.3 %collective-permute-start = (f32[145,32,128]{2,1,0:T(8,128)S(1)}, f32[145,32,128]{2,1,0:T(8,128)S(1)}, u32[]{:S(2)}, u32[]{:S(2)}) collective-permute-start(f32[145,32,128]{2,1,0:T(8,128)S(1)} %get-tuple-element.24.own.own_before), channel_id=1, source_target_pairs={{0,1},{1,0},{2,3},{3,2},{4,5},{5,4},{6,7},{7,6},{8,9},{9,8},{10,11... | collective-permute-start | bytes 7127048 | tf_op jit(solution)/shard_map/ppermute | solution.py:790
  7.8 0.0 collective-permute-start.1
  7.8 8.6 %collective-permute-start.2 = (f32[5,32,128]{2,1,0:T(8,128)S(1)}, f32[5,32,128]{2,1,0:T(8,128)S(1)}, u32[]{:S(2)}, u32[]{:S(2)}) collective-permute-start(f32[5,32,128]{2,1,0:T(8,128)S(1)} %get-tuple-element.28), channel_id=1, source_target_pairs={{0,254},{1,255},{2,0},{3,1},{4,2},{5,3},{6,4},{7,5},{8,6},{9,7},{1... | collective-permute-start | bytes 245768 | tf_op jit(solution)/shard_map/ppermute | solution.py:790
  16.4 0.0 collective-permute-done.other.other_before
  16.4 2.9 %plane.1 = (f32[4,27,32,128]{3,2,1,0:T(8,128)S(1)}, s32[8,6]{1,0:T(8,128)S(1)}) custom-call(s32[4]{0:T(128)S(1)} %pad_add_fusion.info, s32[1024]{0:T(1024)S(1)} %copy-done.4, s32[4,6]{1,0:T(4,128)S(1)} %copy-done.5, f32[145,32,128]{2,1,0:T(8,128)S(1)} %get-tuple-element.24.own.own_before, f32[145,32,128]{2,1,0:T(8,128)S(1)} %collective-permute-done.other.other_before), custom_call_target="tpu_custom_call" | custom-call | flops 134217728 | bytes 8388608 | tf_op jit(solution)/shard_map/plane/pallas_call | solution.py:816
  19.3 0.0 collective-permute-done.1.up_own
  19.3 0.0 collective-permute-done.2.down_own
  19.3 0.4 collective-permute-start.3
  19.7 0.2 collective-permute-start.4
  19.9 0.8 %collective-permute-done.3.up_other = f32[5,32,128]{2,1,0:T(8,128)S(1)} collective-permute-done((f32[5,32,128]{2,1,0:T(8,128)S(1)}, f32[5,32,128]{2,1,0:T(8,128)S(1)}, u32[]{:S(2)}, u32[]{:S(2)}) %collective-permute-start.3) | collective-permute-done | bytes 81952 | tf_op jit(solution)/shard_map/ppermute | solution.py:790
  20.7 0.3 collective-permute-done.4.down_other
  21.0 0.0 copy-start.2
  21.0 8.4 %middle.1 = (f32[144,32,128]{2,1,0:T(8,128)S(1)}, f32[6,32,128]{2,1,0:T(8,128)S(1)}, f32[6,32,128]{2,1,0:T(8,128)S(1)}, s32[16,6]{1,0:T(8,128)S(1)}) custom-call(s32[4]{0:T(128)S(1)} %pad_add_fusion.info, s32[1024]{0:T(1024)S(1)} %copy-done.4, s32[8,6]{1,0:T(8,128)S(1)} %get-tuple-element.25.near, f32[27]{0:T(128)S(1)} %copy-done.6, f32[9]{0:T(128)S(1)} %copy-done.7, ...), custom_call_target="tpu_custom_call" | custom-call | flops 268435456 | bytes 8388608 | tf_op jit(solution)/shard_map/middle/pallas_call | solution.py:828
  29.3 0.1 collective-permute-start.5
  29.4 0.1 collective-permute-start.6
  29.5 0.0 copy-start
  29.5 0.0 copy-start.1
  29.6 0.0 copy-start.3
  29.6 6.9 %collective-permute-start.7 = (f32[6,32,128]{2,1,0:T(8,128)S(1)}, f32[6,32,128]{2,1,0:T(8,128)S(1)}, u32[]{:S(2)}, u32[]{:S(2)}) collective-permute-start(f32[6,32,128]{2,1,0:T(8,128)S(1)} %get-tuple-element.37), channel_id=1, source_target_pairs={{0,254},{1,255},{2,0},{3,1},{4,2},{5,3},{6,4},{7,5},{8,6},{9,7},{1... | collective-permute-start | bytes 294920 | tf_op jit(solution)/shard_map/ppermute | solution.py:790
  36.4 0.0 collective-permute-done.5.other
  36.4 3.8 %plane2.1 = (f32[4,27,32,128]{3,2,1,0:T(8,128)S(1)}, f32[4,2304]{1,0:T(4,128)S(1)}) custom-call(s32[4]{0:T(128)S(1)} %pad_add_fusion.info, s32[1024]{0:T(1024)S(1)} %copy-done.4, s32[8,6]{1,0:T(8,128)S(1)} %get-tuple-element.25.near, f32[144,32,128]{2,1,0:T(8,128)S(1)} %get-tuple-element.33.own, f32[144,32,128]{2,1,0:T(8,128)S(1)} %collective-permute-done.5.other, ...), custom_call_target="tpu_custom_call" | custom-call | flops 134217728 | bytes 8388608 | tf_op jit(solution)/shard_map/plane2/pallas_call | solution.py:843
  40.2 0.0 collective-permute-done.6.up_own
  40.2 0.0 collective-permute-done.7.down_own
  40.2 2.1 %collective-permute-start.8 = (f32[6,32,128]{2,1,0:T(8,128)S(1)}, f32[6,32,128]{2,1,0:T(8,128)S(1)}, u32[]{:S(2)}, u32[]{:S(2)}) collective-permute-start(f32[6,32,128]{2,1,0:T(8,128)S(1)} %collective-permute-done.6.up_own), channel_id=1, source_target_pairs={{0,1},{1,0},{2,3},{3,2},{4,5},{5,4},{6,7},{7,6},{8,9},{9,8},{10,11... | collective-permute-start | bytes 294920 | tf_op jit(solution)/shard_map/ppermute | solution.py:790
  42.3 0.1 collective-permute-start.9
  42.4 0.8 %collective-permute-done.8.up_other = f32[6,32,128]{2,1,0:T(8,128)S(1)} collective-permute-done((f32[6,32,128]{2,1,0:T(8,128)S(1)}, f32[6,32,128]{2,1,0:T(8,128)S(1)}, u32[]{:S(2)}, u32[]{:S(2)}) %collective-permute-start.8) | collective-permute-done | bytes 98336 | tf_op jit(solution)/shard_map/ppermute | solution.py:790
  43.3 0.4 collective-permute-done.9.down_other
  43.6 6.4 %end.1 = (f32[27,128,128]{2,1,0:T(8,128)}, f32[9,128,128]{2,1,0:T(8,128)}, f32[4,3456]{1,0:T(4,128)}) custom-call(s32[4]{0:T(128)S(1)} %pad_add_fusion.info, s32[1024]{0:T(1024)S(1)} %copy-done.4, s32[4,6]{1,0:T(4,128)S(1)} %copy-done.5, s32[16,6]{1,0:T(8,128)S(1)} %get-tuple-element.32.table, f32[9]{0:T(128)S(1)} %copy-done.7, f32[9]{0:T(128)S(1)} %copy-done.8, ...), custom_call_target="tpu_custom_call" | custom-call | flops 134217728 | bytes 8388608 | tf_op jit(solution)/shard_map/end/pallas_call | solution.py:854
  (12 shorter events, 0.0 us)
Async XLA Ops:
  0.6 15.7 %copy-start.4 = (s32[1024]{0:T(1024)S(1)}, s32[1024]{0:T(1024)}, u32[]{:S(2)}) copy-start(s32[1024]{0:T(1024)} %levels.7) | copy-start | bytes 12292
  0.6 15.7 %copy-start.5 = (s32[4,6]{1,0:T(4,128)S(1)}, s32[4,6]{1,0:T(4,128)}, u32[]{:S(2)}) copy-start(s32[4,6]{1,0:T(4,128)} %near.3) | copy-start | bytes 292
  4.5 11.9 %collective-permute-start = (f32[145,32,128]{2,1,0:T(8,128)S(1)}, f32[145,32,128]{2,1,0:T(8,128)S(1)}, u32[]{:S(2)}, u32[]{:S(2)}) collective-permute-start(f32[145,32,128]{2,1,0:T(8,128)S(1)} %get-tuple-element.24.own.own_before), channel_id=1, source_target_pairs={{0,1},{1,0},{2,3},{3,2},{4,5},{5,4},{6,7},{7,6},{8,9},{9,8},{10,11... | collective-permute-start | bytes 7127048 | tf_op jit(solution)/shard_map/ppermute | solution.py:790
  7.8 11.5 %collective-permute-start.1 = (f32[5,32,128]{2,1,0:T(8,128)S(1)}, f32[5,32,128]{2,1,0:T(8,128)S(1)}, u32[]{:S(2)}, u32[]{:S(2)}) collective-permute-start(f32[5,32,128]{2,1,0:T(8,128)S(1)} %get-tuple-element.27), channel_id=1, source_target_pairs={{0,2},{1,3},{2,4},{3,5},{4,6},{5,7},{6,8},{7,9},{8,10},{9,11},{10,... | collective-permute-start | bytes 245768 | tf_op jit(solution)/shard_map/ppermute | solution.py:790
  7.8 13.2 %copy-start.6 = (f32[27]{0:T(128)S(1)}, f32[27]{0:T(128)}, u32[]{:S(2)}) copy-start(f32[27]{0:T(128)} %rates.1) | copy-start | bytes 328
  7.8 13.2 %copy-start.7 = (f32[9]{0:T(128)S(1)}, f32[9]{0:T(128)}, u32[]{:S(2)}) copy-start(f32[9]{0:T(128)} %diffusivity.3) | copy-start | bytes 112
  7.8 13.2 %copy-start.8 = (f32[9]{0:T(128)S(1)}, f32[9]{0:T(128)}, u32[]{:S(2)}) copy-start(f32[9]{0:T(128)} %stoichiometry.3) | copy-start | bytes 112
  7.8 11.5 %collective-permute-start.2 = (f32[5,32,128]{2,1,0:T(8,128)S(1)}, f32[5,32,128]{2,1,0:T(8,128)S(1)}, u32[]{:S(2)}, u32[]{:S(2)}) collective-permute-start(f32[5,32,128]{2,1,0:T(8,128)S(1)} %get-tuple-element.28), channel_id=1, source_target_pairs={{0,254},{1,255},{2,0},{3,1},{4,2},{5,3},{6,4},{7,5},{8,6},{9,7},{1... | collective-permute-start | bytes 245768 | tf_op jit(solution)/shard_map/ppermute | solution.py:790
  19.3 1.4 %collective-permute-start.3 = (f32[5,32,128]{2,1,0:T(8,128)S(1)}, f32[5,32,128]{2,1,0:T(8,128)S(1)}, u32[]{:S(2)}, u32[]{:S(2)}) collective-permute-start(f32[5,32,128]{2,1,0:T(8,128)S(1)} %collective-permute-done.1.up_own), channel_id=1, source_target_pairs={{0,1},{1,0},{2,3},{3,2},{4,5},{5,4},{6,7},{7,6},{8,9},{9,8},{10,11... | collective-permute-start | bytes 245768 | tf_op jit(solution)/shard_map/ppermute | solution.py:790
  19.7 1.3 %collective-permute-start.4 = (f32[5,32,128]{2,1,0:T(8,128)S(1)}, f32[5,32,128]{2,1,0:T(8,128)S(1)}, u32[]{:S(2)}, u32[]{:S(2)}) collective-permute-start(f32[5,32,128]{2,1,0:T(8,128)S(1)} %collective-permute-done.2.down_own), channel_id=1, source_target_pairs={{0,1},{1,0},{2,3},{3,2},{4,5},{5,4},{6,7},{7,6},{8,9},{9,8},{10,11... | collective-permute-start | bytes 245768 | tf_op jit(solution)/shard_map/ppermute | solution.py:790
  21.0 15.5 %copy-start.2 = (f32[384,640]{1,0:T(8,128)S(1)}, f32[384,640]{1,0:T(8,128)}, u32[]{:S(2)}) copy-start(f32[384,640]{1,0:T(8,128)} %constant.49.clone.tables) | copy-start | bytes 2949124
  29.3 7.1 %collective-permute-start.5 = (f32[144,32,128]{2,1,0:T(8,128)S(1)}, f32[144,32,128]{2,1,0:T(8,128)S(1)}, u32[]{:S(2)}, u32[]{:S(2)}) collective-permute-start(f32[144,32,128]{2,1,0:T(8,128)S(1)} %get-tuple-element.33.own), channel_id=1, source_target_pairs={{0,1},{1,0},{2,3},{3,2},{4,5},{5,4},{6,7},{7,6},{8,9},{9,8},{10,11... | collective-permute-start | bytes 7077896 | tf_op jit(solution)/shard_map/ppermute | solution.py:790
  29.4 10.8 %collective-permute-start.6 = (f32[6,32,128]{2,1,0:T(8,128)S(1)}, f32[6,32,128]{2,1,0:T(8,128)S(1)}, u32[]{:S(2)}, u32[]{:S(2)}) collective-permute-start(f32[6,32,128]{2,1,0:T(8,128)S(1)} %get-tuple-element.36), channel_id=1, source_target_pairs={{0,2},{1,3},{2,4},{3,5},{4,6},{5,7},{6,8},{7,9},{8,10},{9,11},{10,... | collective-permute-start | bytes 294920 | tf_op jit(solution)/shard_map/ppermute | solution.py:790
  29.5 14.1 %copy-start = (f32[4,27,4096]{2,0,1:T(4,128)S(1)}, f32[4,27,4096]{2,0,1:T(4,128)}, u32[]{:S(2)}) copy-start(f32[4,27,4096]{2,0,1:T(4,128)} %param.11) | copy-start | bytes 5308420
  29.5 14.1 %copy-start.1 = (f32[4,9,4096]{2,0,1:T(4,128)S(1)}, f32[4,9,4096]{2,0,1:T(4,128)}, u32[]{:S(2)}) copy-start(f32[4,9,4096]{2,0,1:T(4,128)} %param.12) | copy-start | bytes 1769476
  29.6 14.1 %copy-start.3 = (f32[128,640]{1,0:T(8,128)S(1)}, f32[128,640]{1,0:T(8,128)}, u32[]{:S(2)}) copy-start(f32[128,640]{1,0:T(8,128)} %constant.50.clone.weights) | copy-start | bytes 983044
  29.6 10.6 %collective-permute-start.7 = (f32[6,32,128]{2,1,0:T(8,128)S(1)}, f32[6,32,128]{2,1,0:T(8,128)S(1)}, u32[]{:S(2)}, u32[]{:S(2)}) collective-permute-start(f32[6,32,128]{2,1,0:T(8,128)S(1)} %get-tuple-element.37), channel_id=1, source_target_pairs={{0,254},{1,255},{2,0},{3,1},{4,2},{5,3},{6,4},{7,5},{8,6},{9,7},{1... | collective-permute-start | bytes 294920 | tf_op jit(solution)/shard_map/ppermute | solution.py:790
  40.2 3.0 %collective-permute-start.8 = (f32[6,32,128]{2,1,0:T(8,128)S(1)}, f32[6,32,128]{2,1,0:T(8,128)S(1)}, u32[]{:S(2)}, u32[]{:S(2)}) collective-permute-start(f32[6,32,128]{2,1,0:T(8,128)S(1)} %collective-permute-done.6.up_own), channel_id=1, source_target_pairs={{0,1},{1,0},{2,3},{3,2},{4,5},{5,4},{6,7},{7,6},{8,9},{9,8},{10,11... | collective-permute-start | bytes 294920 | tf_op jit(solution)/shard_map/ppermute | solution.py:790
  42.3 1.3 %collective-permute-start.9 = (f32[6,32,128]{2,1,0:T(8,128)S(1)}, f32[6,32,128]{2,1,0:T(8,128)S(1)}, u32[]{:S(2)}, u32[]{:S(2)}) collective-permute-start(f32[6,32,128]{2,1,0:T(8,128)S(1)} %collective-permute-done.7.down_own), channel_id=1, source_target_pairs={{0,1},{1,0},{2,3},{3,2},{4,5},{5,4},{6,7},{7,6},{8,9},{9,8},{10,11... | collective-permute-start | bytes 294920 | tf_op jit(solution)/shard_map/ppermute | solution.py:790
